TPU v7x, 32 devices: a whole 2x2x4 slice. The times are simulated.
32 devices in a mesh: dp: 8 (over z, y), expert: 2 (over core), tensor: 2 (over x).
Axes of the slice: x: 2, y: 2, z: 4, core: 2. Of those that a mesh axis runs over, the one named last changes fastest.
Arguments:
- dense_act: bfloat16 [2, 32, 512, 3584], P(None, 'dp', 'expert', 'tensor'), may hold values from -6 to 6
- dense_cot: bfloat16 [2, 32, 512, 3584], P(None, 'dp', ('expert', 'tensor')), may hold values from -6 to 6
- dense_proj_in: bfloat16 [2, 3584, 128], P(None, 'tensor'), may hold values from -0.09375 to 0.09375
- dense_proj_out: bfloat16 [2, 3584, 128], replicated, may hold values from -0.09375 to 0.09375
- expert_act: bfloat16 [32, 8, 64, 2560], P('dp', 'expert', None, 'tensor'), may hold values from -6 to 6
- expert_cot: bfloat16 [32, 8, 64, 3584], P('dp', 'expert', 'tensor'), may hold values from -6 to 6
- expert_proj_in: bfloat16 [2560, 128], P('tensor'), may hold values from -0.125 to 0.125
- expert_proj_out: bfloat16 [3584, 128], replicated, may hold values from -0.09375 to 0.09375
- dense_valid: float32 [2, 128, 128], replicated, may hold values from -0.0012207031 to 0.0012207031
- expert_valid: float32 [8, 128, 128], P('expert'), may hold values from -0.0012207031 to 0.0012207031
- domain_ids: int32 [32], P('dp'), may hold values from 0 to 63
- prior_mix: float32 [64], replicated, may hold values from 0.002 to 0.05
Outputs:
- log_mixture_weights: float32 [64], P('dp')
All inputs are finite; a program needn't handle non-finite values.
Results may differ from a plain program's by a relative error of at most 0.0003.
Values sent between devices are 32-bit elements; how exact they have to be, the bound alone decides.
No kernel may reach another device: no remote copies, remote signals or barrier semaphores. Data moves between devices by JAX's collectives and lax.ppermute only.
A program may use at most 128 MiB of HBM per device.

v0:
```python
import jax
import jax.numpy as jnp
from jax import lax
from jax.sharding import PartitionSpec as P


def per_device(
    dense_act,
    dense_cot,
    dense_proj_in,
    dense_proj_out,
    expert_act,
    expert_cot,
    expert_proj_in,
    expert_proj_out,
    dense_valid,
    expert_valid,
    domain_ids,
    prior_mix,
):
    block = dense_act
    dense_update_vector = lax.psum_scatter(
        jnp.einsum("lmtd,ldr->tlmr", block, dense_proj_in, preferred_element_type=jnp.float32),
        "tensor",
        scatter_dimension=0,
        tiled=True,
    )
    dense_weight_matrix = jnp.einsum(
        "lmtd,ldr->tlmr", dense_cot, dense_proj_out, preferred_element_type=jnp.float32
    )
    dense_portion = jnp.einsum(
        "fquy,fquh->quyh", dense_update_vector, dense_weight_matrix, precision=lax.Precision.HIGHEST
    )
    block = expert_act
    expert_u = lax.psum_scatter(
        jnp.einsum("mecf,fr->cmer", block, expert_proj_in, preferred_element_type=jnp.float32),
        "tensor",
        scatter_dimension=0,
        tiled=True,
    )
    expert_weight_matrix = jnp.einsum(
        "mecd,dr->cmer", expert_cot, expert_proj_out, preferred_element_type=jnp.float32
    )
    expert_part = jnp.einsum(
        "cmer,cmes->mers", expert_u, expert_weight_matrix, precision=lax.Precision.HIGHEST
    )
    dense_full = lax.psum(dense_portion, ("expert", "tensor"))
    dense_score = jnp.sum(dense_full * dense_valid[:, None], axis=(0, 2, 3))
    expert_full = lax.psum(expert_part, "tensor")
    expert_local = jnp.sum(expert_full * expert_valid[None], axis=(1, 2, 3))
    score = dense_score + lax.psum(expert_local, "expert")
    domains = prior_mix.shape[0]
    onehot = (domain_ids[:, None] == jnp.arange(domains, dtype=jnp.int32)[None, :]).astype(
        jnp.float32
    )
    domain_part = jnp.dot(score, onehot, precision=lax.Precision.HIGHEST)
    share_tally_count = domains // lax.axis_size("dp")
    first_domain = lax.axis_index("dp") * share_tally_count
    previous_domain_share = lax.dynamic_slice_in_dim(prior_mix, first_domain, share_tally_count, 0)
    domain_total = lax.psum(domain_part, "dp")
    spread = jnp.sqrt(jnp.mean(domain_total * domain_total) + 1e-06)
    z_value = domain_total / spread
    mass = jnp.sum(prior_mix * jnp.exp(0.5 * z_value))
    z_share = lax.dynamic_slice_in_dim(z_value, first_domain, share_tally_count, 0)
    return jnp.log(previous_domain_share) + 0.5 * z_share - jnp.log(mass)


def solution(mesh):
    placed = (
        P(None, "dp", "expert", "tensor"),
        P(None, "dp", ("expert", "tensor"), None),
        P(None, "tensor", None),
        P(),
        P("dp", "expert", None, "tensor"),
        P("dp", "expert", "tensor", None),
        P("tensor", None),
        P(),
        P(),
        P("expert", None, None),
        P("dp"),
        P(),
    )
    return jax.shard_map(per_device, mesh=mesh, in_specs=placed, out_specs=P("dp"), check_vma=False)
```

profile of v0, /device:TPU:0, one launch (start us, length us, event | category | flops | bytes accessed | tf_op | source)
XLA Modules:
  0.0 206.4 jit_solution(693878961875852554)
XLA Ops:
  6.5 0.0 copy-start
  6.5 0.0 copy-start.3
  6.5 0.0 all-reduce.9.cloned.1.call-start
  6.5 1.7 copy-done
  8.3 1.8 convolution_bitcast_fusion.1
  10.1 1.1 copy.18
  11.2 0.0 all-reduce.9.cloned.1.call-update
  11.3 0.0 reduce-scatter.4.cloned.1.call-start
  11.3 0.0 copy-done.3
  11.3 5.6 %convolution_bitcast_fusion = f32[256,2,4,128]{0,3,2,1:T(8,128)S(1)} fusion(bf16[2,4,256,1792]{3,2,1,0:T(8,128)(2,1)} %param.12, bf16[2,1792,128]{2,1,0:T(8,128)(2,1)S(1)} %copy-done.3), kind=kOutput, calls=%fused_computation.2 | convolution fusion | flops 939524096 | bytes 9306112 | tf_op jit(solution)/shard_map/lmtd,ldr->tlmr/dot_general | solution.py:23
  16.9 26.2 %copy.29 = f32[256,2,4,128]{2,3,1,0:T(8,128)} copy(f32[256,2,4,128]{0,3,2,1:T(8,128)S(1)} %convolution_bitcast_fusion) | data formatting | bytes 2097152
  43.2 0.0 copy-start.9
  43.2 0.0 copy-start.7
  43.2 29.4 %reshape.9 = f32[256,1024]{1,0:T(8,128)} reshape(f32[256,2,128,4]{3,2,1,0:T(8,128)} %bitcast.46) | data formatting | bytes 2097152
  72.5 0.0 reduce-scatter.4.cloned.1.call-update
  72.6 0.0 all-reduce.7.cloned.1.call-start
  72.6 0.0 copy-done.9
  72.6 0.6 dynamic-slice
  73.9 0.0 copy-done.7
  73.9 0.0 copy-start.2
  73.9 3.3 %fusion.6 = f32[128,4,4,32]{0,3,2,1:T(8,128)S(1)} fusion(bf16[4,4,32,3584]{3,2,1,0:T(8,128)(2,1)} %param.17, bf16[3584,128]{1,0:T(8,128)(2,1)S(1)} %copy-done.7), kind=kOutput, calls=%fused_computation.8 | convolution fusion | flops 469762048 | bytes 4849664 | tf_op jit(solution)/shard_map/mecd,dr->cmer/dot_general | solution.py:41
  77.2 0.0 all-reduce.9.cloned.1.call-done
  77.2 1.0 constant_dynamic-slice_fusion
  78.2 2.8 %fusion.9 = f32[4,4,128,128]{3,2,1,0:T(8,128)} fusion(f32[128,4,4,32]{0,3,2,1:T(8,128)S(1)} %fusion.6, f32[32,4,4,128]{3,2,1,0:T(4,128)S(1)} %constant_dynamic-slice_fusion), kind=kOutput, calls=%fused_computation.12 | convolution fusion | flops 100663296 | bytes 1572864 | tf_op jit(solution)/shard_map/cmer,cmes->mers/dot_general | solution.py:44
  81.0 0.0 all-reduce.7.cloned.1.call-update
  81.0 0.2 all-reduce.5.cloned.1.call-start
  81.3 0.0 copy-done.2
  81.3 5.6 %fusion.2 = f32[128,2,4,128]{0,3,2,1:T(8,128)S(1)} fusion(bf16[2,4,128,3584]{3,2,1,0:T(8,128)(2,1)} %param.13, bf16[2,3584,128]{2,1,0:T(8,128)(2,1)S(1)} %copy-done.2), kind=kOutput, calls=%fused_computation.3 | convolution fusion | flops 939524096 | bytes 9699328 | tf_op jit(solution)/shard_map/lmtd,ldr->tlmr/dot_general | solution.py:28
  86.9 8.9 %reduce-scatter.4.cloned.1.call-done = f32[128,1024]{1,0:T(8,128)} async-done(((f32[256,1024]{1,0:T(8,128)}), f32[128,1024]{1,0:T(8,128)}) %reduce-scatter.4.cloned.1.call-update) | async-done | bytes 524304
  95.8 19.5 %reshape.10 = f32[128,2,128,4]{3,2,1,0:T(8,128)} reshape(f32[128,1024]{1,0:T(8,128)} %reduce-scatter.4.cloned.1.call-done) | data formatting | bytes 1048576
  115.3 13.2 %copy.16 = f32[128,2,4,128]{0,3,2,1:T(8,128)} copy(f32[128,2,4,128]{2,3,1,0:T(8,128)} %bitcast.47) | data formatting | bytes 1048576 | tf_op jit(solution)/shard_map/reduce_scatter | solution.py:22
  128.5 3.1 %fusion.12 = f32[2,4,128,128]{3,2,1,0:T(8,128)} fusion(f32[128,2,4,128]{0,3,2,1:T(8,128)} %copy.16, f32[128,2,4,128]{0,3,2,1:T(8,128)S(1)} %fusion.2), kind=kOutput, calls=%fused_computation.22 | convolution fusion | flops 201326592 | bytes 1572864 | tf_op jit(solution)/shard_map/fquy,fquh->quyh/dot_general | solution.py:31
  131.6 0.0 all-reduce.5.cloned.1.call-update
  131.6 6.7 %all-reduce.7.cloned.1.call-done = f32[4,4,128,128]{3,2,1,0:T(8,128)} async-done(((f32[4,4,128,128]{3,2,1,0:T(8,128)}), f32[4,4,128,128]{3,2,1,0:T(8,128)}) %all-reduce.7.cloned.1.call-update) | async-done | bytes 1048592 | tf_op jit(solution)/shard_map/psum | solution.py:49
  138.3 0.0 copy-done.4
  138.3 1.4 multiply_reduce_fusion
  139.7 2.4 %psum.30 = f32[4]{0:T(128)S(1)} all-reduce(f32[4]{0:T(128)S(1)} %multiply_reduce_fusion), channel_id=1, replica_groups=mesh['dp'=8,'expert'=2,'tensor'=2] {'expert'}, use_global_device_ids=true, to_apply=%region_6.0 | all-reduce | flops 4 | bytes 32 | tf_op jit(solution)/shard_map/psum | solution.py:51
  142.1 31.8 %all-reduce.5.cloned.1.call-done = f32[2,4,128,128]{3,2,1,0:T(8,128)} async-done(((f32[2,4,128,128]{3,2,1,0:T(8,128)}), f32[2,4,128,128]{3,2,1,0:T(8,128)}) %all-reduce.5.cloned.1.call-update) | async-done | bytes 524304 | tf_op jit(solution)/shard_map/psum | solution.py:47
  173.9 0.0 copy-done.5
  173.9 1.2 multiply_reduce_fusion.1
  175.1 0.0 copy-done.8
  175.1 0.2 convolution_bitcast_fusion.2
  175.3 21.3 %psum.31 = f32[64]{0:T(128)S(1)} all-reduce(f32[64]{0:T(128)S(1)} %convolution_bitcast_fusion.2), channel_id=1, replica_groups=mesh['dp'=8,'expert'=2,'tensor'=2] {'dp'}, use_global_device_ids=true, to_apply=%region_7.0 | all-reduce | flops 64 | bytes 512 | tf_op jit(solution)/shard_map/psum | solution.py:60
  196.7 0.6 multiply_reduce_fusion.3
  198.0 0.0 copy-done.6
  198.0 0.6 multiply_reduce_fusion.2
  199.3 0.6 add_subtract_fusion
  199.9 0.0 copy-done.1
  (5 shorter events, 0.0 us)
Async XLA Ops:
  6.5 1.7 copy-start
  6.5 4.8 %copy-start.3 = (bf16[2,1792,128]{2,1,0:T(8,128)(2,1)S(1)}, bf16[2,1792,128]{2,1,0:T(8,128)(2,1)}, u32[]{:S(2)}) copy-start(bf16[2,1792,128]{2,1,0:T(8,128)(2,1)} %param.14) | copy-start | bytes 2752516
  6.5 70.6 %all-reduce.9.cloned.1.call-start = ((), (), s32[]{:S(2)}) async-start(), calls=%async_computation.4 | async-start | bytes 1048576
  11.3 84.6 %reduce-scatter.4.cloned.1.call-start = ((), (), s32[]{:S(2)}) async-start(), calls=%async_computation.3 | async-start | bytes 1572864
  43.2 29.4 %copy-start.9 = (u32[32]{0:T(128)S(1)}, u32[32]{0:T(128)}, u32[]{:S(2)}) copy-start(u32[32]{0:T(128)} %constant.29) | copy-start | bytes 388
  43.2 30.7 %copy-start.7 = (bf16[3584,128]{1,0:T(8,128)(2,1)S(1)}, bf16[3584,128]{1,0:T(8,128)(2,1)}, u32[]{:S(2)}) copy-start(bf16[3584,128]{1,0:T(8,128)(2,1)} %param.19) | copy-start | bytes 2752516
  72.6 65.7 %all-reduce.7.cloned.1.call-start = ((), (), s32[]{:S(2)}) async-start(), calls=%async_computation.2 | async-start | bytes 2097152 | tf_op jit(solution)/shard_map/psum | solution.py:49
  73.9 7.4 %copy-start.2 = (bf16[2,3584,128]{2,1,0:T(8,128)(2,1)S(1)}, bf16[2,3584,128]{2,1,0:T(8,128)(2,1)}, u32[]{:S(2)}) copy-start(bf16[2,3584,128]{2,1,0:T(8,128)(2,1)} %param.15) | copy-start | bytes 5505028
  81.0 92.9 %all-reduce.5.cloned.1.call-start = ((), (), s32[]{:S(2)}) async-start(), calls=%async_computation.1 | async-start | bytes 1048576 | tf_op jit(solution)/shard_map/psum | solution.py:47
  115.3 22.9 %copy-start.4 = (f32[4,128,128]{2,1,0:T(8,128)S(1)}, f32[4,128,128]{2,1,0:T(8,128)}, u32[]{:S(2)}) copy-start(f32[4,128,128]{2,1,0:T(8,128)} %param.21) | copy-start | bytes 786436
  115.3 58.6 %copy-start.5 = (f32[2,128,128]{2,1,0:T(8,128)S(1)}, f32[2,128,128]{2,1,0:T(8,128)}, u32[]{:S(2)}) copy-start(f32[2,128,128]{2,1,0:T(8,128)} %param.20) | copy-start | bytes 393220
  115.3 84.5 %copy-start.1 = (bf16[4,4,64,1280]{3,2,1,0:T(8,128)(2,1)S(1)}, bf16[4,4,64,1280]{3,2,1,0:T(8,128)(2,1)}, u32[]{:S(2)}) copy-start(bf16[4,4,64,1280]{3,2,1,0:T(8,128)(2,1)} %param.16) | copy-start | bytes 7864324
  128.5 46.6 %copy-start.8 = (s32[4]{0:T(128)S(1)}, s32[4]{0:T(128)}, u32[]{:S(2)}) copy-start(s32[4]{0:T(128)} %param.22) | copy-start | bytes 52
  128.5 69.5 %copy-start.6 = (f32[64]{0:T(128)S(1)}, f32[64]{0:T(128)}, u32[]{:S(2)}) copy-start(f32[64]{0:T(128)} %param.23) | copy-start | bytes 772
Sparse Core Ops, SparseCore 0:
  11.4 31.3 all-reduce.8
  72.7 23.1 reduce-scatter.3
  98.1 40.0 all-reduce.6
  140.5 33.4 all-reduce.4
where the time goes:
time: 207 us; the launch traced here: 206 us
  local copies, waits for them, and re-layouts  92.7 us (45%)
  waiting for transfers between devices  47.4 us (23%)
  blocking collectives  23.8 us (11%)
  matrix products  22.5 us (11%)
  between operations  15.3 us (7%)
  other arithmetic  4.44 us (2%)
    unnamed x25, local copies, waits for them, and re-layouts  78.4 us
    psum x1, waiting for transfers between devices, per_device(): dense_full = lax.psum(dense_portion, ('expert', 'tensor'))  31.8 us
    psum x1, blocking collectives, per_device(): domain_total = lax.psum(domain_part, 'dp')  21.3 us
    reduce_scatter x1, local copies, waits for them, and re-layouts, per_device(): lax.psum_scatter(jnp.einsum('lmtd,ldr->tlmr', block, dense_proj_in, prefe...  13.2 us
    unnamed x6, waiting for transfers between devices  8.98 us
    psum x1, waiting for transfers between devices, per_device(): expert_full = lax.psum(expert_part, 'tensor')  6.66 us
    dot_general x1, matrix products, per_device(): jnp.einsum('lmtd,ldr->tlmr', dense_cot, dense_proj_out, preferred_element...  5.64 us
    dot_general x1, matrix products, per_device(): jnp.einsum('lmtd,ldr->tlmr', block, dense_proj_in, preferred_element_type...  5.62 us
  transfers between devices with their start and end apart: 4, of which 3 were waited for; matrix products, arithmetic and copies ran while one was open for 54% of the time, Pallas kernels for 0%

commit v1 on v0

v1 whole, which is shorter than its diff:
```python
import functools

import jax
import jax.numpy as jnp
from jax import lax
from jax.experimental import pallas as pl
from jax.experimental.pallas import tpu as pltpu
from jax.sharding import PartitionSpec as P


AXES = ("dp", "expert", "tensor")
HBM = pl.BlockSpec(memory_space=pltpu.HBM)
ANY = pl.BlockSpec(memory_space=pl.ANY)
VMEM = pl.BlockSpec(memory_space=pltpu.VMEM)
SMEM = pl.BlockSpec(memory_space=pltpu.SMEM)


def vmem(mib):
    return pltpu.CompilerParams(vmem_limit_bytes=mib * 2**20)


def start_all(pairs, sems):
    copies = [pltpu.make_async_copy(src, dst, sems.at[i]) for i, (src, dst) in enumerate(pairs)]
    for copy in copies:
        copy.start()
    return copies


def dot(a, b):
    return jnp.dot(a, b, preferred_element_type=jnp.float32)


def dot_exact(a, b):
    return lax.dot_general(
        a, b, (((1,), (1,)), ((), ())), precision=lax.Precision.HIGHEST, preferred_element_type=jnp.float32
    )


def expert_send_kernel(act, proj, out, act_v, proj_v, sems):
    micro, experts, rows, width = act_v.shape
    first = (1 - lax.axis_index("tensor")) * rows
    copies = start_all(
        [(proj, proj_v)] + [(act.at[m, :, pl.ds(first, rows), :], act_v.at[m]) for m in range(micro)], sems
    )
    copies[0].wait()
    for m in range(micro):
        copies[1 + m].wait()
        u = dot(act_v[m].reshape(experts * rows, width), proj_v[...])
        out[m] = u.reshape(experts, rows, -1)


def dense_send_kernel(act, proj, _after, out, act_v, proj_v, sems):
    layers, micro, rows, _ = act_v.shape
    first = (1 - lax.axis_index("tensor")) * rows
    pairs = []
    for l in range(layers):
        pairs.append((proj.at[l], proj_v.at[l]))
        pairs += [(act.at[l, m, pl.ds(first, rows), :], act_v.at[l, m]) for m in range(micro)]
    copies = start_all(pairs, sems)
    for l in range(layers):
        copies[l * (micro + 1)].wait()
        for m in range(micro):
            copies[l * (micro + 1) + 1 + m].wait()
            out[l, m] = dot(act_v[l, m], proj_v[l])


def own_kernel(
    dact, dcot, dpin, dpout, eact, ecot, epin, epout, dval, evaldn,
    yd, ye, own,
    dact_v, dcot_v, dpin_v, dpout_v, eact_v, ecot_v, epin_v, epout_v, dval_v, eval_v, sems,
):
    layers, micro, rows, _ = dact_v.shape
    _, experts, slots, ewidth = eact_v.shape
    rank = dval_v.shape[-1]
    tensor = lax.axis_index("tensor")
    pairs = []
    for l in range(layers):
        pairs += [(dpout.at[l], dpout_v.at[l]), (dval.at[l], dval_v.at[l]), (dpin.at[l], dpin_v.at[l])]
        for m in range(micro):
            pairs += [
                (dcot.at[l, m], dcot_v.at[l, m]),
                (dact.at[l, m, pl.ds(tensor * rows, rows), :], dact_v.at[l, m]),
            ]
    pairs += [(epout, epout_v), (evaldn, eval_v), (epin, epin_v)]
    for m in range(micro):
        pairs += [
            (ecot.at[m], ecot_v.at[m]),
            (eact.at[m, :, pl.ds(tensor * slots, slots), :], eact_v.at[m]),
        ]
    copies = iter(start_all(pairs, sems))
    totals = [jnp.zeros((1, rank), jnp.float32) for _ in range(micro)]
    for l in range(layers):
        for _ in range(3):
            next(copies).wait()
        for m in range(micro):
            next(copies).wait()
            w = dot(dcot_v[l, m], dpout_v[l])
            y = dot_exact(w, dval_v[l])
            yd[l, m] = y
            next(copies).wait()
            u = dot(dact_v[l, m], dpin_v[l])
            totals[m] = totals[m] + jnp.sum(u * y, axis=0, keepdims=True)
    for _ in range(3):
        next(copies).wait()
    for m in range(micro):
        next(copies).wait()
        w = dot(ecot_v[m].reshape(experts * slots, -1), epout_v[...])
        next(copies).wait()
        u = dot(eact_v[m].reshape(experts * slots, ewidth), epin_v[...])
        for e in range(experts):
            part = slice(e * slots, (e + 1) * slots)
            y = dot_exact(w[part], eval_v[e])
            ye[m, e] = y
            totals[m] = totals[m] + jnp.sum(u[part] * y, axis=0, keepdims=True)
    own[...] = jnp.concatenate(totals, axis=0)


def combine_kernel(ids, own, ud, yd, ue, ye, out):
    layers, micro = ud.shape[:2]
    domains = out.shape[-1]
    lane = lax.broadcasted_iota(jnp.int32, (1, domains), 1)
    total = jnp.zeros((1, domains), jnp.float32)
    for m in range(micro):
        part = own[pl.ds(m, 1), :]
        for l in range(layers):
            part = part + jnp.sum(ud[l, m] * yd[l, m], axis=0, keepdims=True)
        experts, slots, rank = ue.shape[1:]
        e_prod = ue[m].reshape(experts * slots, rank) * ye[m].reshape(experts * slots, rank)
        part = part + jnp.sum(e_prod, axis=0, keepdims=True)
        score = jnp.sum(part, axis=1, keepdims=True)
        total = total + jnp.where(lane == ids[m], score, 0.0)
    out[...] = jnp.broadcast_to(total, out.shape)


def final_kernel(parts, prior, out, wide):
    domains = prior.shape[-1]
    share = out.shape[-1]
    total = jnp.sum(parts[...], axis=0, keepdims=True)
    spread = jnp.sqrt(jnp.mean(total * total, axis=1, keepdims=True) + 1e-06)
    half = 0.5 * (total / spread)
    mass = jnp.sum(prior[...] * jnp.exp(half), axis=1, keepdims=True)
    lanes = wide.shape[-1]
    wide[...] = jnp.zeros_like(wide)
    wide[:, :domains] = jnp.log(prior[...]) + half - jnp.log(mass)
    first = lax.axis_index("dp") * share
    out[...] = pltpu.roll(wide[...], lax.rem(lanes - first, lanes), 1)[:, :share]


def per_device(
    dense_act,
    dense_cot,
    dense_proj_in,
    dense_proj_out,
    expert_act,
    expert_cot,
    expert_proj_in,
    expert_proj_out,
    dense_valid,
    expert_valid,
    domain_ids,
    prior_mix,
):
    layers, micro, rows, dwidth = dense_cot.shape
    experts, slots = expert_cot.shape[1:3]
    d_in = dense_act.shape[3]
    e_in = expert_act.shape[3]
    rank = dense_proj_in.shape[2]
    domains = prior_mix.shape[0]
    world = lax.axis_size(AXES)
    n_tensor = lax.axis_size("tensor")
    swap = [(i, i ^ 1) for i in range(n_tensor)]
    f32, bf16 = jnp.float32, jnp.bfloat16
    dma = pltpu.SemaphoreType.DMA

    hbm = functools.partial(pltpu.with_memory_space_constraint, memory_space=pltpu.HBM)
    dense_act, dense_cot, dense_proj_in, dense_proj_out = map(
        hbm, (dense_act, dense_cot, dense_proj_in, dense_proj_out)
    )
    expert_act, expert_cot, expert_proj_in, expert_proj_out = map(
        hbm, (expert_act, expert_cot, expert_proj_in, expert_proj_out)
    )
    dense_valid, expert_valid = hbm(dense_valid), hbm(expert_valid)

    e_send = pl.pallas_call(
        expert_send_kernel,
        out_shape=jax.ShapeDtypeStruct((micro, experts, slots, rank), f32),
        in_specs=[HBM, HBM],
        out_specs=VMEM,
        scratch_shapes=[
            pltpu.VMEM((micro, experts, slots, e_in), bf16),
            pltpu.VMEM((e_in, rank), bf16),
            dma((micro + 1,)),
        ],
        compiler_params=vmem(4),
        name="expert_send",
    )(expert_act, expert_proj_in)
    e_got = lax.ppermute(e_send, "tensor", swap)

    d_send = pl.pallas_call(
        dense_send_kernel,
        out_shape=jax.ShapeDtypeStruct((layers, micro, rows, rank), f32),
        in_specs=[HBM, HBM, ANY],
        out_specs=VMEM,
        scratch_shapes=[
            pltpu.VMEM((layers, micro, rows, d_in), bf16),
            pltpu.VMEM((layers, d_in, rank), bf16),
            dma((layers * (micro + 1),)),
        ],
        compiler_params=vmem(8),
        name="dense_send",
    )(dense_act, dense_proj_in, e_send)
    d_got = lax.ppermute(d_send, "tensor", swap)

    y_d, y_e, own = pl.pallas_call(
        own_kernel,
        out_shape=[
            jax.ShapeDtypeStruct((layers, micro, rows, rank), f32),
            jax.ShapeDtypeStruct((micro, experts, slots, rank), f32),
            jax.ShapeDtypeStruct((micro, rank), f32),
        ],
        in_specs=[HBM] * 10,
        out_specs=[VMEM] * 3,
        scratch_shapes=[
            pltpu.VMEM((layers, micro, rows, d_in), bf16),
            pltpu.VMEM((layers, micro, rows, dwidth), bf16),
            pltpu.VMEM((layers, d_in, rank), bf16),
            pltpu.VMEM((layers, dwidth, rank), bf16),
            pltpu.VMEM((micro, experts, slots, e_in), bf16),
            pltpu.VMEM((micro, experts, slots, dwidth), bf16),
            pltpu.VMEM((e_in, rank), bf16),
            pltpu.VMEM((dwidth, rank), bf16),
            pltpu.VMEM((layers, rank, rank), f32),
            pltpu.VMEM((experts, rank, rank), f32),
            dma((layers * (3 + 2 * micro) + 3 + 2 * micro,)),
        ],
        compiler_params=vmem(32),
        name="own_part",
    )(
        dense_act, dense_cot, dense_proj_in, dense_proj_out,
        expert_act, expert_cot, expert_proj_in, expert_proj_out, dense_valid, expert_valid,
    )

    parts = pl.pallas_call(
        combine_kernel,
        out_shape=jax.ShapeDtypeStruct((world, domains), f32),
        in_specs=[SMEM] + [VMEM] * 5,
        out_specs=VMEM,
        compiler_params=vmem(6),
        name="combine",
    )(domain_ids, own, d_got, y_d, e_got, y_e)
    parts = lax.all_to_all(parts, AXES, 0, 0, tiled=True)

    share = domains // lax.axis_size("dp")
    lanes = -(-domains // 128) * 128
    out = pl.pallas_call(
        final_kernel,
        out_shape=jax.ShapeDtypeStruct((1, share), f32),
        in_specs=[VMEM, VMEM],
        out_specs=VMEM,
        scratch_shapes=[pltpu.VMEM((1, lanes), f32)],
        compiler_params=vmem(1),
        name="final",
    )(parts, prior_mix.reshape(1, domains))
    return out.reshape(share)


def solution(mesh):
    placed = (
        P(None, "dp", "expert", "tensor"),
        P(None, "dp", ("expert", "tensor"), None),
        P(None, "tensor", None),
        P(),
        P("dp", "expert", None, "tensor"),
        P("dp", "expert", "tensor", None),
        P("tensor", None),
        P(),
        P(),
        P("expert", None, None),
        P("dp"),
        P(),
    )

    return jax.shard_map(per_device, mesh=mesh, in_specs=placed, out_specs=P("dp"), check_vma=False)
```

time: 207 us -> 41.1 us (0.20)
  local copies, waits for them, and re-layouts: 92.7 us -> 0.01 us
  waiting for transfers between devices: 47.4 us -> 3.31 us
  matrix products: 22.5 us -> 0 us
  Pallas kernels: 0 us -> 21.4 us
  between operations: 15.3 us -> 0.04 us
  blocking collectives: 23.8 us -> 13.1 us
  other arithmetic: 4.44 us -> 0 us
  starting transfers between devices: 0.31 us -> 3.11 us
    unnamed x25 -> x4, local copies, waits for them, and re-layouts: 78.4 us -> 0.01 us
    psum x2 -> x0, waiting for transfers between devices: 38.4 us -> none  [the longest x1 31.8 us: per_device(): dense_full = lax.psum(dense_portion, ('expert', 'tensor'))]
    psum x2 -> x0, blocking collectives: 23.8 us -> none  [the longest x1 21.3 us: per_device(): domain_total = lax.psum(domain_part, 'dp')]
    dot_general x7 -> x0, matrix products: 22.5 us -> none  [the longest x1 5.64 us: per_device(): jnp.einsum('lmtd,ldr->tlmr', dense_cot, dense_proj_out, preferred_element...]
    pallas_call x0 -> x5, Pallas kernels: none -> 21.4 us  [the longest x1 14.1 us: per_device(): pl.pallas_call(own_kernel, out_shape=[jax.ShapeDtypeStruct((layers, micro...]
    reduce_scatter x1 -> x0, local copies, waits for them, and re-layouts: 13.2 us -> none  [per_device(): lax.psum_scatter(jnp.einsum('lmtd,ldr->tlmr', block, dense_proj_in, prefe...]
    all_to_all x0 -> x1, blocking collectives: none -> 13.1 us  [per_device(): parts = lax.all_to_all(parts, AXES, 0, 0, tiled=True)]
    unnamed x6 -> x0, waiting for transfers between devices: 8.98 us -> none
  transfers between devices with their start and end apart: 4 -> 2, of which waited for: 3 -> 1; matrix products, arithmetic and copies ran while one was open for 54% -> 0% of each run, Pallas kernels for 0% -> 35%
where the time goes in v1:
time: 41.1 us; the launch traced here: 40.9 us
  Pallas kernels  21.4 us (52%)
  blocking collectives  13.1 us (32%)
  waiting for transfers between devices  3.31 us (8%)
  starting transfers between devices  3.11 us (8%)
    pallas_call x1, Pallas kernels, per_device(): pl.pallas_call(own_kernel, out_shape=[jax.ShapeDtypeStruct((layers, micro...  14.1 us
    all_to_all x1, blocking collectives, per_device(): parts = lax.all_to_all(parts, AXES, 0, 0, tiled=True)  13.1 us
    pallas_call x1, Pallas kernels, per_device(): pl.pallas_call(dense_send_kernel, out_shape=jax.ShapeDtypeStruct((layers,...  3.55 us
    ppermute x1, waiting for transfers between devices, per_device(): e_got = lax.ppermute(e_send, 'tensor', swap)  3.3 us
    ppermute x1, starting transfers between devices, per_device(): d_got = lax.ppermute(d_send, 'tensor', swap)  3.03 us
    pallas_call x1, Pallas kernels, per_device(): pl.pallas_call(expert_send_kernel, out_shape=jax.ShapeDtypeStruct((micro,...  2.13 us
  transfers between devices with their start and end apart: 2, of which 1 were waited for; matrix products, arithmetic and copies ran while one was open for 0% of the time, Pallas kernels for 35%

profile of v1, /device:TPU:0, one launch (start us, length us, event | category | flops | bytes accessed | tf_op | source)
XLA Modules:
  0.0 40.9 jit_solution(10198350225379007727)
XLA Ops:
  0.0 2.1 %expert_send.1._after = f32[4,4,32,128]{3,2,1,0:T(8,128)S(1)} custom-call(bf16[4,4,64,1280]{3,2,1,0:T(8,128)(2,1)} %act.2, bf16[1280,128]{1,0:T(8,128)(2,1)} %proj.2), custom_call_target="tpu_custom_call" | custom-call | tf_op jit(solution)/shard_map/expert_send/pallas_call | solution.py:184
  2.1 3.6 %dense_send.1 = f32[2,4,128,128]{3,2,1,0:T(8,128)S(1)} custom-call(bf16[2,4,256,1792]{3,2,1,0:T(8,128)(2,1)} %act.3, bf16[2,1792,128]{2,1,0:T(8,128)(2,1)} %proj.3, f32[4,4,32,128]{3,2,1,0:T(8,128)S(1)} %expert_send.1._after), custom_call_target="tpu_custom_call" | custom-call | tf_op jit(solution)/shard_map/dense_send/pallas_call | solution.py:199
  5.7 0.0 copy-start
  5.7 0.0 copy-start.1
  5.7 3.0 %collective-permute-start = (f32[2,4,128,128]{3,2,1,0:T(8,128)S(1)}, f32[2,4,128,128]{3,2,1,0:T(8,128)S(1)}, u32[]{:S(2)}, u32[]{:S(2)}) collective-permute-start(f32[2,4,128,128]{3,2,1,0:T(8,128)S(1)} %dense_send.1), channel_id=1, source_target_pairs={{0,1},{1,0},{2,3},{3,2},{4,5},{5,4},{6,7},{7,6},{8,9},{9,8},{10,11... | collective-permute-start | bytes 1572872 | tf_op jit(solution)/shard_map/ppermute | solution.py:212
  8.8 0.1 collective-permute-start.1
  8.8 14.1 %own_part.1 = (f32[2,4,128,128]{3,2,1,0:T(8,128)S(1)}, f32[4,4,32,128]{3,2,1,0:T(8,128)S(1)}, f32[4,128]{1,0:T(4,128)S(1)}) custom-call(bf16[2,4,256,1792]{3,2,1,0:T(8,128)(2,1)} %act.3, bf16[2,4,128,3584]{3,2,1,0:T(8,128)(2,1)} %dcot.1, bf16[2,1792,128]{2,1,0:T(8,128)(2,1)} %proj.3, bf16[2,3584,128]{2,1,0:T(8,128)(2,1)} %dpout.1, ...), custom_call_target="tpu_custom_call" | custom-call | tf_op jit(solution)/shard_map/own_part/pallas_call | solution.py:214
  23.0 3.3 %collective-permute-done.1.ue = f32[4,4,32,128]{3,2,1,0:T(8,128)S(1)} collective-permute-done((f32[4,4,32,128]{3,2,1,0:T(8,128)S(1)}, f32[4,4,32,128]{3,2,1,0:T(8,128)S(1)}, u32[]{:S(2)}, u32[]{:S(2)}) %collective-permute-start.1) | collective-permute-done | bytes 262176 | tf_op jit(solution)/shard_map/ppermute | solution.py:197
  26.3 0.0 collective-permute-done.ud
  26.3 0.0 copy-done
  26.3 0.7 %combine.1 = f32[32,64]{1,0:T(8,128)S(1)} custom-call(s32[4]{0:T(128)S(1)} %copy-done, f32[4,128]{1,0:T(4,128)S(1)} %get-tuple-element.8.own, f32[2,4,128,128]{3,2,1,0:T(8,128)S(1)} %collective-permute-done.ud, f32[2,4,128,128]{3,2,1,0:T(8,128)S(1)} %get-tuple-element.9.yd, f32[4,4,32,128]{3,2,1,0:T(8,128)S(1)} %collective-permute-done.1.ue, ...), custom_call_target="tpu_custom_call" | custom-call | tf_op jit(solution)/shard_map/combine/pallas_call | solution.py:243
  27.0 13.1 %all_to_all.11 = f32[32,1,64]{2,1,0:T(1,128)S(1)} all-to-all(f32[32,1,64]{2,1,0:T(1,128)S(1)} %bitcast.6), channel_id=1, replica_groups=mesh['dp'=8,'expert'=2,'tensor'=2] {'dp','expert','tensor'}, dimensions={0} | all-to-all | bytes 16384 | tf_op jit(solution)/shard_map/all_to_all | solution.py:251
  40.2 0.0 copy-done.1
  40.2 0.8 %final.1 = f32[1,8]{1,0:T(1,128)} custom-call(f32[32,64]{1,0:T(8,128)S(1)} %bitcast.7, f32[1,64]{1,0:T(1,128)S(1)} %bitcast.8), custom_call_target="tpu_custom_call" | custom-call | tf_op jit(solution)/shard_map/final/pallas_call | solution.py:255
Async XLA Ops:
  5.7 20.6 %copy-start = (s32[4]{0:T(128)S(1)}, s32[4]{0:T(128)}, u32[]{:S(2)}) copy-start(s32[4]{0:T(128)} %ids.1) | copy-start | bytes 52
  5.7 34.5 %copy-start.1 = (f32[64]{0:T(128)S(1)}, f32[64]{0:T(128)}, u32[]{:S(2)}) copy-start(f32[64]{0:T(128)} %param.23) | copy-start | bytes 772
  5.7 20.6 %collective-permute-start = (f32[2,4,128,128]{3,2,1,0:T(8,128)S(1)}, f32[2,4,128,128]{3,2,1,0:T(8,128)S(1)}, u32[]{:S(2)}, u32[]{:S(2)}) collective-permute-start(f32[2,4,128,128]{3,2,1,0:T(8,128)S(1)} %dense_send.1), channel_id=1, source_target_pairs={{0,1},{1,0},{2,3},{3,2},{4,5},{5,4},{6,7},{7,6},{8,9},{9,8},{10,11... | collective-permute-start | bytes 1572872 | tf_op jit(solution)/shard_map/ppermute | solution.py:212
  8.8 17.5 %collective-permute-start.1 = (f32[4,4,32,128]{3,2,1,0:T(8,128)S(1)}, f32[4,4,32,128]{3,2,1,0:T(8,128)S(1)}, u32[]{:S(2)}, u32[]{:S(2)}) collective-permute-start(f32[4,4,32,128]{3,2,1,0:T(8,128)S(1)} %expert_send.1._after), channel_id=1, source_target_pairs={{0,1},{1,0},{2,3},{3,2},{4,5},{5,4},{6,7},{7,6},{8,9},{9,8},{10,11... | collective-permute-start | bytes 786440 | tf_op jit(solution)/shard_map/ppermute | solution.py:197

commit v2 on v1

--- a/solution.py
+++ b/solution.py
@@ -42,26 +42,24 @@
     copies = start_all(
         [(proj, proj_v)] + [(act.at[m, :, pl.ds(first, rows), :], act_v.at[m]) for m in range(micro)], sems
     )
-    copies[0].wait()
-    for m in range(micro):
-        copies[1 + m].wait()
-        u = dot(act_v[m].reshape(experts * rows, width), proj_v[...])
-        out[m] = u.reshape(experts, rows, -1)
+    for copy in copies:
+        copy.wait()
+    u = dot(act_v[...].reshape(micro * experts * rows, width), proj_v[...])
+    out[...] = u.reshape(out.shape)
 
 
 def dense_send_kernel(act, proj, _after, out, act_v, proj_v, sems):
-    layers, micro, rows, _ = act_v.shape
+    layers, micro, rows, width = act_v.shape
     first = (1 - lax.axis_index("tensor")) * rows
     pairs = []
     for l in range(layers):
         pairs.append((proj.at[l], proj_v.at[l]))
         pairs += [(act.at[l, m, pl.ds(first, rows), :], act_v.at[l, m]) for m in range(micro)]
-    copies = start_all(pairs, sems)
-    for l in range(layers):
-        copies[l * (micro + 1)].wait()
-        for m in range(micro):
-            copies[l * (micro + 1) + 1 + m].wait()
-            out[l, m] = dot(act_v[l, m], proj_v[l])
+    copies = iter(start_all(pairs, sems))
+    for l in range(layers):
+        for _ in range(1 + micro):
+            next(copies).wait()
+        out[l] = dot(act_v[l].reshape(micro * rows, width), proj_v[l]).reshape(micro, rows, -1)
 
 
 def own_kernel(
@@ -69,11 +67,16 @@
     yd, ye, own,
     dact_v, dcot_v, dpin_v, dpout_v, eact_v, ecot_v, epin_v, epout_v, dval_v, eval_v, sems,
 ):
-    layers, micro, rows, _ = dact_v.shape
+    layers, micro, rows, dwidth = dact_v.shape
     _, experts, slots, ewidth = eact_v.shape
     rank = dval_v.shape[-1]
     tensor = lax.axis_index("tensor")
-    pairs = []
+    pairs = [(epout, epout_v), (evaldn, eval_v), (epin, epin_v)]
+    for m in range(micro):
+        pairs += [
+            (ecot.at[m], ecot_v.at[m]),
+            (eact.at[m, :, pl.ds(tensor * slots, slots), :], eact_v.at[m]),
+        ]
     for l in range(layers):
         pairs += [(dpout.at[l], dpout_v.at[l]), (dval.at[l], dval_v.at[l]), (dpin.at[l], dpin_v.at[l])]
         for m in range(micro):
@@ -81,37 +84,29 @@
                 (dcot.at[l, m], dcot_v.at[l, m]),
                 (dact.at[l, m, pl.ds(tensor * rows, rows), :], dact_v.at[l, m]),
             ]
-    pairs += [(epout, epout_v), (evaldn, eval_v), (epin, epin_v)]
-    for m in range(micro):
-        pairs += [
-            (ecot.at[m], ecot_v.at[m]),
-            (eact.at[m, :, pl.ds(tensor * slots, slots), :], eact_v.at[m]),
-        ]
     copies = iter(start_all(pairs, sems))
     totals = [jnp.zeros((1, rank), jnp.float32) for _ in range(micro)]
-    for l in range(layers):
-        for _ in range(3):
+    for _ in range(3 + 2 * micro):
+        next(copies).wait()
+    w = dot(ecot_v[...].reshape(micro * experts * slots, -1), epout_v[...])
+    u = dot(eact_v[...].reshape(micro * experts * slots, ewidth), epin_v[...])
+    for e in range(experts):
+        places = [slice((m * experts + e) * slots, (m * experts + e + 1) * slots) for m in range(micro)]
+        y = dot_exact(jnp.concatenate([w[place] for place in places], axis=0), eval_v[e])
+        for m in range(micro):
+            y_m = y[m * slots : (m + 1) * slots]
+            ye[m, e] = y_m
+            totals[m] = totals[m] + jnp.sum(u[places[m]] * y_m, axis=0, keepdims=True)
+    for l in range(layers):
+        for _ in range(3 + 2 * micro):
             next(copies).wait()
+        w = dot(dcot_v[l].reshape(micro * rows, -1), dpout_v[l])
+        u = dot(dact_v[l].reshape(micro * rows, dwidth), dpin_v[l])
+        y = dot_exact(w, dval_v[l])
         for m in range(micro):
-            next(copies).wait()
-            w = dot(dcot_v[l, m], dpout_v[l])
-            y = dot_exact(w, dval_v[l])
-            yd[l, m] = y
-            next(copies).wait()
-            u = dot(dact_v[l, m], dpin_v[l])
-            totals[m] = totals[m] + jnp.sum(u * y, axis=0, keepdims=True)
-    for _ in range(3):
-        next(copies).wait()
-    for m in range(micro):
-        next(copies).wait()
-        w = dot(ecot_v[m].reshape(experts * slots, -1), epout_v[...])
-        next(copies).wait()
-        u = dot(eact_v[m].reshape(experts * slots, ewidth), epin_v[...])
-        for e in range(experts):
-            part = slice(e * slots, (e + 1) * slots)
-            y = dot_exact(w[part], eval_v[e])
-            ye[m, e] = y
-            totals[m] = totals[m] + jnp.sum(u[part] * y, axis=0, keepdims=True)
+            place = slice(m * rows, (m + 1) * rows)
+            yd[l, m] = y[place]
+            totals[m] = totals[m] + jnp.sum(u[place] * y[place], axis=0, keepdims=True)
     own[...] = jnp.concatenate(totals, axis=0)
 
 

time: 41.1 us -> 41.2 us (level)
  waiting for transfers between devices: 3.31 us -> 6.59 us
  Pallas kernels: 21.4 us -> 18.2 us
    pallas_call x1, Pallas kernels: 14.1 us -> 10.9 us  [per_device(): pl.pallas_call(own_kernel, out_shape=[jax.ShapeDtypeStruct((layers, micro...]
    ppermute x1, waiting for transfers between devices: 3.3 us -> 6.59 us  [per_device(): e_got = lax.ppermute(e_send, 'tensor', swap)]
  transfers between devices with their start and end apart: 2 -> 2, of which waited for: 1 -> 1; matrix products, arithmetic and copies ran while one was open for 0% -> 0% of each run, Pallas kernels for 35% -> 27%
where the time goes in v2:
time: 41.2 us; the launch traced here: 41 us
  Pallas kernels  18.2 us (44%)
  blocking collectives  13.1 us (32%)
  waiting for transfers between devices  6.59 us (16%)
  starting transfers between devices  3.11 us (8%)
    all_to_all x1, blocking collectives, per_device(): parts = lax.all_to_all(parts, AXES, 0, 0, tiled=True)  13.1 us
    pallas_call x1, Pallas kernels, per_device(): pl.pallas_call(own_kernel, out_shape=[jax.ShapeDtypeStruct((layers, micro...  10.9 us
    ppermute x1, waiting for transfers between devices, per_device(): e_got = lax.ppermute(e_send, 'tensor', swap)  6.59 us
    pallas_call x1, Pallas kernels, per_device(): pl.pallas_call(dense_send_kernel, out_shape=jax.ShapeDtypeStruct((layers,...  3.86 us
    ppermute x1, starting transfers between devices, per_device(): d_got = lax.ppermute(d_send, 'tensor', swap)  3.03 us
    pallas_call x1, Pallas kernels, per_device(): pl.pallas_call(expert_send_kernel, out_shape=jax.ShapeDtypeStruct((micro,...  1.91 us
  transfers between devices with their start and end apart: 2, of which 1 were waited for; matrix products, arithmetic and copies ran while one was open for 0% of the time, Pallas kernels for 27%

profile of v2, /device:TPU:0, one launch (start us, length us, event | category | flops | bytes accessed | tf_op | source)
XLA Modules:
  0.0 41.0 jit_solution(13502783631549195455)
XLA Ops:
  0.0 1.9 %expert_send.1._after = f32[4,4,32,128]{3,2,1,0:T(8,128)S(1)} custom-call(bf16[4,4,64,1280]{3,2,1,0:T(8,128)(2,1)} %act.2, bf16[1280,128]{1,0:T(8,128)(2,1)} %proj.2), custom_call_target="tpu_custom_call" | custom-call | tf_op jit(solution)/shard_map/expert_send/pallas_call | solution.py:179
  1.9 3.9 %dense_send.1 = f32[2,4,128,128]{3,2,1,0:T(8,128)S(1)} custom-call(bf16[2,4,256,1792]{3,2,1,0:T(8,128)(2,1)} %act.3, bf16[2,1792,128]{2,1,0:T(8,128)(2,1)} %proj.3, f32[4,4,32,128]{3,2,1,0:T(8,128)S(1)} %expert_send.1._after), custom_call_target="tpu_custom_call" | custom-call | tf_op jit(solution)/shard_map/dense_send/pallas_call | solution.py:194
  5.8 0.0 copy-start
  5.8 0.0 copy-start.1
  5.8 3.0 %collective-permute-start = (f32[2,4,128,128]{3,2,1,0:T(8,128)S(1)}, f32[2,4,128,128]{3,2,1,0:T(8,128)S(1)}, u32[]{:S(2)}, u32[]{:S(2)}) collective-permute-start(f32[2,4,128,128]{3,2,1,0:T(8,128)S(1)} %dense_send.1), channel_id=1, source_target_pairs={{0,1},{1,0},{2,3},{3,2},{4,5},{5,4},{6,7},{7,6},{8,9},{9,8},{10,11... | collective-permute-start | bytes 1572872 | tf_op jit(solution)/shard_map/ppermute | solution.py:207
  8.8 0.1 collective-permute-start.1
  8.9 10.9 %own_part.1 = (f32[2,4,128,128]{3,2,1,0:T(8,128)S(1)}, f32[4,4,32,128]{3,2,1,0:T(8,128)S(1)}, f32[4,128]{1,0:T(4,128)S(1)}) custom-call(bf16[2,4,256,1792]{3,2,1,0:T(8,128)(2,1)} %act.3, bf16[2,4,128,3584]{3,2,1,0:T(8,128)(2,1)} %dcot.1, bf16[2,1792,128]{2,1,0:T(8,128)(2,1)} %proj.3, bf16[2,3584,128]{2,1,0:T(8,128)(2,1)} %dpout.1, ...), custom_call_target="tpu_custom_call" | custom-call | tf_op jit(solution)/shard_map/own_part/pallas_call | solution.py:209
  19.8 6.6 %collective-permute-done.1.ue = f32[4,4,32,128]{3,2,1,0:T(8,128)S(1)} collective-permute-done((f32[4,4,32,128]{3,2,1,0:T(8,128)S(1)}, f32[4,4,32,128]{3,2,1,0:T(8,128)S(1)}, u32[]{:S(2)}, u32[]{:S(2)}) %collective-permute-start.1) | collective-permute-done | bytes 262176 | tf_op jit(solution)/shard_map/ppermute | solution.py:192
  26.4 0.0 collective-permute-done.ud
  26.4 0.0 copy-done
  26.4 0.7 %combine.1 = f32[32,64]{1,0:T(8,128)S(1)} custom-call(s32[4]{0:T(128)S(1)} %copy-done, f32[4,128]{1,0:T(4,128)S(1)} %get-tuple-element.8.own, f32[2,4,128,128]{3,2,1,0:T(8,128)S(1)} %collective-permute-done.ud, f32[2,4,128,128]{3,2,1,0:T(8,128)S(1)} %get-tuple-element.9.yd, f32[4,4,32,128]{3,2,1,0:T(8,128)S(1)} %collective-permute-done.1.ue, ...), custom_call_target="tpu_custom_call" | custom-call | tf_op jit(solution)/shard_map/combine/pallas_call | solution.py:238
  27.1 13.1 %all_to_all.11 = f32[32,1,64]{2,1,0:T(1,128)S(1)} all-to-all(f32[32,1,64]{2,1,0:T(1,128)S(1)} %bitcast.6), channel_id=1, replica_groups=mesh['dp'=8,'expert'=2,'tensor'=2] {'dp','expert','tensor'}, dimensions={0} | all-to-all | bytes 16384 | tf_op jit(solution)/shard_map/all_to_all | solution.py:246
  40.3 0.0 copy-done.1
  40.3 0.8 %final.1 = f32[1,8]{1,0:T(1,128)} custom-call(f32[32,64]{1,0:T(8,128)S(1)} %bitcast.7, f32[1,64]{1,0:T(1,128)S(1)} %bitcast.8), custom_call_target="tpu_custom_call" | custom-call | tf_op jit(solution)/shard_map/final/pallas_call | solution.py:250
Async XLA Ops:
  5.8 20.6 %copy-start = (s32[4]{0:T(128)S(1)}, s32[4]{0:T(128)}, u32[]{:S(2)}) copy-start(s32[4]{0:T(128)} %ids.1) | copy-start | bytes 52
  5.8 34.5 %copy-start.1 = (f32[64]{0:T(128)S(1)}, f32[64]{0:T(128)}, u32[]{:S(2)}) copy-start(f32[64]{0:T(128)} %param.23) | copy-start | bytes 772
  5.8 20.6 %collective-permute-start = (f32[2,4,128,128]{3,2,1,0:T(8,128)S(1)}, f32[2,4,128,128]{3,2,1,0:T(8,128)S(1)}, u32[]{:S(2)}, u32[]{:S(2)}) collective-permute-start(f32[2,4,128,128]{3,2,1,0:T(8,128)S(1)} %dense_send.1), channel_id=1, source_target_pairs={{0,1},{1,0},{2,3},{3,2},{4,5},{5,4},{6,7},{7,6},{8,9},{9,8},{10,11... | collective-permute-start | bytes 1572872 | tf_op jit(solution)/shard_map/ppermute | solution.py:207
  8.8 17.5 %collective-permute-start.1 = (f32[4,4,32,128]{3,2,1,0:T(8,128)S(1)}, f32[4,4,32,128]{3,2,1,0:T(8,128)S(1)}, u32[]{:S(2)}, u32[]{:S(2)}) collective-permute-start(f32[4,4,32,128]{3,2,1,0:T(8,128)S(1)} %expert_send.1._after), channel_id=1, source_target_pairs={{0,1},{1,0},{2,3},{3,2},{4,5},{5,4},{6,7},{7,6},{8,9},{9,8},{10,11... | collective-permute-start | bytes 786440 | tf_op jit(solution)/shard_map/ppermute | solution.py:192

commit v3 on v2

--- a/solution.py
+++ b/solution.py
@@ -63,8 +63,8 @@
 
 
 def own_kernel(
-    dact, dcot, dpin, dpout, eact, ecot, epin, epout, dval, evaldn,
-    yd, ye, own,
+    ids, dact, dcot, dpin, dpout, eact, ecot, epin, epout, dval, evaldn,
+    yd, ye, own, hot,
     dact_v, dcot_v, dpin_v, dpout_v, eact_v, ecot_v, epin_v, epout_v, dval_v, eval_v, sems,
 ):
     layers, micro, rows, dwidth = dact_v.shape
@@ -108,22 +108,23 @@
             yd[l, m] = y[place]
             totals[m] = totals[m] + jnp.sum(u[place] * y[place], axis=0, keepdims=True)
     own[...] = jnp.concatenate(totals, axis=0)
-
-
-def combine_kernel(ids, own, ud, yd, ue, ye, out):
+    lane = lax.broadcasted_iota(jnp.int32, (1, hot.shape[1]), 1)
+    for m in range(micro):
+        hot[pl.ds(m, 1), :] = (lane == ids[m]).astype(jnp.float32)
+
+
+def combine_kernel(own, hot, ud, yd, ue, ye, out):
     layers, micro = ud.shape[:2]
-    domains = out.shape[-1]
-    lane = lax.broadcasted_iota(jnp.int32, (1, domains), 1)
-    total = jnp.zeros((1, domains), jnp.float32)
+    parts = []
     for m in range(micro):
         part = own[pl.ds(m, 1), :]
         for l in range(layers):
             part = part + jnp.sum(ud[l, m] * yd[l, m], axis=0, keepdims=True)
         experts, slots, rank = ue.shape[1:]
         e_prod = ue[m].reshape(experts * slots, rank) * ye[m].reshape(experts * slots, rank)
-        part = part + jnp.sum(e_prod, axis=0, keepdims=True)
-        score = jnp.sum(part, axis=1, keepdims=True)
-        total = total + jnp.where(lane == ids[m], score, 0.0)
+        parts.append(part + jnp.sum(e_prod, axis=0, keepdims=True))
+    scores = jnp.sum(jnp.concatenate(parts, axis=0), axis=1, keepdims=True)
+    total = jnp.sum(scores * hot[...], axis=0, keepdims=True)
     out[...] = jnp.broadcast_to(total, out.shape)
 
 
@@ -206,15 +207,16 @@
     )(dense_act, dense_proj_in, e_send)
     d_got = lax.ppermute(d_send, "tensor", swap)
 
-    y_d, y_e, own = pl.pallas_call(
+    y_d, y_e, own, hot = pl.pallas_call(
         own_kernel,
         out_shape=[
             jax.ShapeDtypeStruct((layers, micro, rows, rank), f32),
             jax.ShapeDtypeStruct((micro, experts, slots, rank), f32),
             jax.ShapeDtypeStruct((micro, rank), f32),
-        ],
-        in_specs=[HBM] * 10,
-        out_specs=[VMEM] * 3,
+            jax.ShapeDtypeStruct((micro, domains), f32),
+        ],
+        in_specs=[SMEM] + [HBM] * 10,
+        out_specs=[VMEM] * 4,
         scratch_shapes=[
             pltpu.VMEM((layers, micro, rows, d_in), bf16),
             pltpu.VMEM((layers, micro, rows, dwidth), bf16),
@@ -231,18 +233,18 @@
         compiler_params=vmem(32),
         name="own_part",
     )(
-        dense_act, dense_cot, dense_proj_in, dense_proj_out,
+        domain_ids, dense_act, dense_cot, dense_proj_in, dense_proj_out,
         expert_act, expert_cot, expert_proj_in, expert_proj_out, dense_valid, expert_valid,
     )
 
     parts = pl.pallas_call(
         combine_kernel,
         out_shape=jax.ShapeDtypeStruct((world, domains), f32),
-        in_specs=[SMEM] + [VMEM] * 5,
+        in_specs=[VMEM] * 6,
         out_specs=VMEM,
         compiler_params=vmem(6),
         name="combine",
-    )(domain_ids, own, d_got, y_d, e_got, y_e)
+    )(own, hot, d_got, y_d, e_got, y_e)
     parts = lax.all_to_all(parts, AXES, 0, 0, tiled=True)
 
     share = domains // lax.axis_size("dp")

time: 41.2 us -> 40.7 us (0.988)
  waiting for transfers between devices: 6.59 us -> 6.04 us
    ppermute x1, waiting for transfers between devices: 6.59 us -> 6.04 us  [per_device(): e_got = lax.ppermute(e_send, 'tensor', swap)]
    pallas_call x1, Pallas kernels: 10.9 us -> 11.4 us  [per_device(): pl.pallas_call(own_kernel, out_shape=[jax.ShapeDtypeStruct((layers, micro...]
    pallas_call x1, Pallas kernels: 0.74 us -> 0.2 us  [per_device(): pl.pallas_call(combine_kernel, out_shape=jax.ShapeDtypeStruct((world, dom...]
  transfers between devices with their start and end apart: 2 -> 2, of which waited for: 1 -> 1; matrix products, arithmetic and copies ran while one was open for 0% -> 0% of each run, Pallas kernels for 27% -> 28%
where the time goes in v3:
time: 40.7 us; the launch traced here: 40.5 us
  Pallas kernels  18.2 us (45%)
  blocking collectives  13.1 us (32%)
  waiting for transfers between devices  6.04 us (15%)
  starting transfers between devices  3.11 us (8%)
    all_to_all x1, blocking collectives, per_device(): parts = lax.all_to_all(parts, AXES, 0, 0, tiled=True)  13.1 us
    pallas_call x1, Pallas kernels, per_device(): pl.pallas_call(own_kernel, out_shape=[jax.ShapeDtypeStruct((layers, micro...  11.4 us
    ppermute x1, waiting for transfers between devices, per_device(): e_got = lax.ppermute(e_send, 'tensor', swap)  6.04 us
    pallas_call x1, Pallas kernels, per_device(): pl.pallas_call(dense_send_kernel, out_shape=jax.ShapeDtypeStruct((layers,...  3.86 us
    ppermute x1, starting transfers between devices, per_device(): d_got = lax.ppermute(d_send, 'tensor', swap)  3.03 us
    pallas_call x1, Pallas kernels, per_device(): pl.pallas_call(expert_send_kernel, out_shape=jax.ShapeDtypeStruct((micro,...  1.91 us
  transfers between devices with their start and end apart: 2, of which 1 were waited for; matrix products, arithmetic and copies ran while one was open for 0% of the time, Pallas kernels for 28%

profile of v3, /device:TPU:0, one launch (start us, length us, event | category | flops | bytes accessed | tf_op | source)
XLA Modules:
  0.0 40.5 jit_solution(12204952824610524760)
XLA Ops:
  0.0 1.9 %expert_send.1._after = f32[4,4,32,128]{3,2,1,0:T(8,128)S(1)} custom-call(bf16[4,4,64,1280]{3,2,1,0:T(8,128)(2,1)} %act.2, bf16[1280,128]{1,0:T(8,128)(2,1)} %proj.2), custom_call_target="tpu_custom_call" | custom-call | tf_op jit(solution)/shard_map/expert_send/pallas_call | solution.py:180
  1.9 0.0 copy-start
  1.9 3.9 %dense_send.1 = f32[2,4,128,128]{3,2,1,0:T(8,128)S(1)} custom-call(bf16[2,4,256,1792]{3,2,1,0:T(8,128)(2,1)} %act.3, bf16[2,1792,128]{2,1,0:T(8,128)(2,1)} %proj.3, f32[4,4,32,128]{3,2,1,0:T(8,128)S(1)} %expert_send.1._after), custom_call_target="tpu_custom_call" | custom-call | tf_op jit(solution)/shard_map/dense_send/pallas_call | solution.py:195
  5.8 0.0 copy-start.1
  5.8 3.0 %collective-permute-start = (f32[2,4,128,128]{3,2,1,0:T(8,128)S(1)}, f32[2,4,128,128]{3,2,1,0:T(8,128)S(1)}, u32[]{:S(2)}, u32[]{:S(2)}) collective-permute-start(f32[2,4,128,128]{3,2,1,0:T(8,128)S(1)} %dense_send.1), channel_id=1, source_target_pairs={{0,1},{1,0},{2,3},{3,2},{4,5},{5,4},{6,7},{7,6},{8,9},{9,8},{10,11... | collective-permute-start | bytes 1572872 | tf_op jit(solution)/shard_map/ppermute | solution.py:208
  8.8 0.1 collective-permute-start.1
  8.9 0.0 copy-done
  8.9 11.4 %own_part.1 = (f32[2,4,128,128]{3,2,1,0:T(8,128)S(1)}, f32[4,4,32,128]{3,2,1,0:T(8,128)S(1)}, f32[4,128]{1,0:T(4,128)S(1)}, f32[4,64]{1,0:T(4,128)S(1)}) custom-call(s32[4]{0:T(128)S(1)} %copy-done, bf16[2,4,256,1792]{3,2,1,0:T(8,128)(2,1)} %act.3, bf16[2,4,128,3584]{3,2,1,0:T(8,128)(2,1)} %dcot.1, bf16[2,1792,128]{2,1,0:T(8,128)(2,1)} %proj.3, ...), custom_call_target="tpu_custom_call" | custom-call | tf_op jit(solution)/shard_map/own_part/pallas_call | solution.py:210
  20.3 6.0 %collective-permute-done.1.ue = f32[4,4,32,128]{3,2,1,0:T(8,128)S(1)} collective-permute-done((f32[4,4,32,128]{3,2,1,0:T(8,128)S(1)}, f32[4,4,32,128]{3,2,1,0:T(8,128)S(1)}, u32[]{:S(2)}, u32[]{:S(2)}) %collective-permute-start.1) | collective-permute-done | bytes 262176 | tf_op jit(solution)/shard_map/ppermute | solution.py:193
  26.4 0.0 collective-permute-done.ud
  26.4 0.2 combine.1
  26.6 13.1 %all_to_all.11 = f32[32,1,64]{2,1,0:T(1,128)S(1)} all-to-all(f32[32,1,64]{2,1,0:T(1,128)S(1)} %bitcast.6), channel_id=1, replica_groups=mesh['dp'=8,'expert'=2,'tensor'=2] {'dp','expert','tensor'}, dimensions={0} | all-to-all | bytes 16384 | tf_op jit(solution)/shard_map/all_to_all | solution.py:248
  39.7 0.0 copy-done.1
  39.7 0.8 %final.1 = f32[1,8]{1,0:T(1,128)} custom-call(f32[32,64]{1,0:T(8,128)S(1)} %bitcast.7, f32[1,64]{1,0:T(1,128)S(1)} %bitcast.8), custom_call_target="tpu_custom_call" | custom-call | tf_op jit(solution)/shard_map/final/pallas_call | solution.py:252
Async XLA Ops:
  1.9 7.0 %copy-start = (s32[4]{0:T(128)S(1)}, s32[4]{0:T(128)}, u32[]{:S(2)}) copy-start(s32[4]{0:T(128)} %ids.1) | copy-start | bytes 52
  5.8 33.9 %copy-start.1 = (f32[64]{0:T(128)S(1)}, f32[64]{0:T(128)}, u32[]{:S(2)}) copy-start(f32[64]{0:T(128)} %param.23) | copy-start | bytes 772
  5.8 20.6 %collective-permute-start = (f32[2,4,128,128]{3,2,1,0:T(8,128)S(1)}, f32[2,4,128,128]{3,2,1,0:T(8,128)S(1)}, u32[]{:S(2)}, u32[]{:S(2)}) collective-permute-start(f32[2,4,128,128]{3,2,1,0:T(8,128)S(1)} %dense_send.1), channel_id=1, source_target_pairs={{0,1},{1,0},{2,3},{3,2},{4,5},{5,4},{6,7},{7,6},{8,9},{9,8},{10,11... | collective-permute-start | bytes 1572872 | tf_op jit(solution)/shard_map/ppermute | solution.py:208
  8.8 17.5 %collective-permute-start.1 = (f32[4,4,32,128]{3,2,1,0:T(8,128)S(1)}, f32[4,4,32,128]{3,2,1,0:T(8,128)S(1)}, u32[]{:S(2)}, u32[]{:S(2)}) collective-permute-start(f32[4,4,32,128]{3,2,1,0:T(8,128)S(1)} %expert_send.1._after), channel_id=1, source_target_pairs={{0,1},{1,0},{2,3},{3,2},{4,5},{5,4},{6,7},{7,6},{8,9},{9,8},{10,11... | collective-permute-start | bytes 786440 | tf_op jit(solution)/shard_map/ppermute | solution.py:193

commit v4 on v3

v4 whole, which is shorter than its diff:
```python
import functools

import jax
import jax.numpy as jnp
from jax import lax
from jax.experimental import pallas as pl
from jax.experimental.pallas import tpu as pltpu
from jax.sharding import PartitionSpec as P


AXES = ("dp", "expert", "tensor")
GROUP = 2
HBM = pl.BlockSpec(memory_space=pltpu.HBM)
ANY = pl.BlockSpec(memory_space=pl.ANY)
VMEM = pl.BlockSpec(memory_space=pltpu.VMEM)
SMEM = pl.BlockSpec(memory_space=pltpu.SMEM)


def vmem(mib):
    return pltpu.CompilerParams(vmem_limit_bytes=mib * 2**20)


def start_all(pairs, sems):
    copies = [pltpu.make_async_copy(src, dst, sems.at[i]) for i, (src, dst) in enumerate(pairs)]
    for copy in copies:
        copy.start()
    return copies


def dot(a, b):
    return jnp.dot(a, b, preferred_element_type=jnp.float32)


def dot_exact(a, b):
    return lax.dot_general(
        a, b, (((1,), (1,)), ((), ())), precision=lax.Precision.HIGHEST, preferred_element_type=jnp.float32
    )


def send_kernel(pieces, e_act, e_proj, d_act, d_proj, *rest):
    n = len(pieces)
    sems = rest[-1]
    acts, projs = rest[-1 - 2 * n : -1 - n], rest[-1 - n : -1]
    out = rest[-2 - 2 * n]
    other = 1 - lax.axis_index("tensor")
    pairs = []
    for (layer, first, many), act_v, proj_v in zip(pieces, acts, projs):
        rows = act_v.shape[-2]
        here = pl.ds(other * rows, rows)
        if layer is None:
            pairs += [(e_proj, proj_v), (e_act.at[pl.ds(first, many), :, here, :], act_v)]
        else:
            pairs += [(d_proj.at[layer], proj_v), (d_act.at[layer, pl.ds(first, many), here, :], act_v)]
    copies = iter(start_all(pairs, sems))
    start = 0
    for act_v, proj_v in zip(acts, projs):
        next(copies).wait()
        next(copies).wait()
        u = dot(act_v[...].reshape(-1, act_v.shape[-1]), proj_v[...])
        out[start : start + u.shape[0], :] = u
        start += u.shape[0]


def own_kernel(
    ids, dact, dcot, dpin, dpout, eact, ecot, epin, epout, dval, evaldn,
    yd, ye, own, hot,
    dact_v, dcot_v, dpin_v, dpout_v, eact_v, ecot_v, epin_v, epout_v, dval_v, eval_v, sems,
):
    layers, micro, rows, dwidth = dact_v.shape
    _, experts, slots, ewidth = eact_v.shape
    rank = dval_v.shape[-1]
    tensor = lax.axis_index("tensor")
    groups = [pl.ds(g, GROUP) for g in range(0, micro, GROUP)]
    pairs = [(epout, epout_v), (evaldn, eval_v), (epin, epin_v)]
    for g in groups:
        pairs += [
            (ecot.at[g], ecot_v.at[g]),
            (eact.at[g, :, pl.ds(tensor * slots, slots), :], eact_v.at[g]),
        ]
    for l in range(layers):
        pairs += [(dpout.at[l], dpout_v.at[l]), (dval.at[l], dval_v.at[l]), (dpin.at[l], dpin_v.at[l])]
        for g in groups:
            pairs += [
                (dcot.at[l, g], dcot_v.at[l, g]),
                (dact.at[l, g, pl.ds(tensor * rows, rows), :], dact_v.at[l, g]),
            ]
    copies = iter(start_all(pairs, sems))
    totals = [jnp.zeros((1, rank), jnp.float32) for _ in range(micro)]
    for _ in range(3):
        next(copies).wait()
    for first in range(0, micro, GROUP):
        next(copies).wait()
        w = dot(ecot_v[first : first + GROUP].reshape(GROUP * experts * slots, -1), epout_v[...])
        next(copies).wait()
        u = dot(eact_v[first : first + GROUP].reshape(GROUP * experts * slots, ewidth), epin_v[...])
        for e in range(experts):
            places = [slice((m * experts + e) * slots, (m * experts + e + 1) * slots) for m in range(GROUP)]
            y = dot_exact(jnp.concatenate([w[place] for place in places], axis=0), eval_v[e])
            for m in range(GROUP):
                y_m = y[m * slots : (m + 1) * slots]
                ye[first + m, e] = y_m
                totals[first + m] = totals[first + m] + jnp.sum(u[places[m]] * y_m, axis=0, keepdims=True)
    for l in range(layers):
        for _ in range(3):
            next(copies).wait()
        for first in range(0, micro, GROUP):
            next(copies).wait()
            w = dot(dcot_v[l, first : first + GROUP].reshape(GROUP * rows, -1), dpout_v[l])
            next(copies).wait()
            u = dot(dact_v[l, first : first + GROUP].reshape(GROUP * rows, dwidth), dpin_v[l])
            y = dot_exact(w, dval_v[l])
            for m in range(GROUP):
                place = slice(m * rows, (m + 1) * rows)
                yd[l, first + m] = y[place]
                totals[first + m] = totals[first + m] + jnp.sum(u[place] * y[place], axis=0, keepdims=True)
    own[...] = jnp.concatenate(totals, axis=0)
    lane = lax.broadcasted_iota(jnp.int32, (1, hot.shape[1]), 1)
    for m in range(micro):
        hot[pl.ds(m, 1), :] = (lane == ids[m]).astype(jnp.float32)


def combine_kernel(chunks, own, hot, yd, ye, *rest):
    *got, out = rest
    micro, _ = yd.shape[1:3]
    experts, slots, rank = ye.shape[1:]
    parts = [own[pl.ds(m, 1), :] for m in range(micro)]
    for pieces, u in zip(chunks, got):
        start = 0
        for layer, first, many in pieces:
            for m in range(first, first + many):
                y = ye[m].reshape(experts * slots, rank) if layer is None else yd[layer, m]
                part = u[start : start + y.shape[0], :] * y
                parts[m] = parts[m] + jnp.sum(part, axis=0, keepdims=True)
                start += y.shape[0]
    scores = jnp.sum(jnp.concatenate(parts, axis=0), axis=1, keepdims=True)
    total = jnp.sum(scores * hot[...], axis=0, keepdims=True)
    out[...] = jnp.broadcast_to(total, out.shape)


def final_kernel(parts, prior, out, wide):
    domains = prior.shape[-1]
    share = out.shape[-1]
    total = jnp.sum(parts[...], axis=0, keepdims=True)
    spread = jnp.sqrt(jnp.mean(total * total, axis=1, keepdims=True) + 1e-06)
    half = 0.5 * (total / spread)
    mass = jnp.sum(prior[...] * jnp.exp(half), axis=1, keepdims=True)
    lanes = wide.shape[-1]
    wide[...] = jnp.zeros_like(wide)
    wide[:, :domains] = jnp.log(prior[...]) + half
    first = lax.axis_index("dp") * share
    rolled = pltpu.roll(wide[...], lax.rem(lanes - first, lanes), 1)
    out[...] = rolled[:, :share] - jnp.log(mass)


def per_device(
    dense_act,
    dense_cot,
    dense_proj_in,
    dense_proj_out,
    expert_act,
    expert_cot,
    expert_proj_in,
    expert_proj_out,
    dense_valid,
    expert_valid,
    domain_ids,
    prior_mix,
):
    layers, micro, rows, dwidth = dense_cot.shape
    experts, slots = expert_cot.shape[1:3]
    d_in = dense_act.shape[3]
    e_in = expert_act.shape[3]
    rank = dense_proj_in.shape[2]
    domains = prior_mix.shape[0]
    world = lax.axis_size(AXES)
    n_tensor = lax.axis_size("tensor")
    swap = [(i, i ^ 1) for i in range(n_tensor)]
    f32, bf16 = jnp.float32, jnp.bfloat16
    dma = pltpu.SemaphoreType.DMA

    hbm = functools.partial(pltpu.with_memory_space_constraint, memory_space=pltpu.HBM)
    dense_act, dense_cot, dense_proj_in, dense_proj_out = map(
        hbm, (dense_act, dense_cot, dense_proj_in, dense_proj_out)
    )
    expert_act, expert_cot, expert_proj_in, expert_proj_out = map(
        hbm, (expert_act, expert_cot, expert_proj_in, expert_proj_out)
    )
    dense_valid, expert_valid = hbm(dense_valid), hbm(expert_valid)

    half = micro // 2
    chunks = [
        [(None, 0, half)],
        [(None, half, micro - half), (0, 0, half)],
        [(0, half, micro - half)] + [(l, 0, micro) for l in range(1, layers)],
    ]
    got = []
    after = []
    for pieces in chunks:
        n_rows = sum(many * (experts * slots if layer is None else rows) for layer, _, many in pieces)
        acts = [
            pltpu.VMEM((many, experts, slots, e_in) if layer is None else (many, rows, d_in), bf16)
            for layer, _, many in pieces
        ]
        projs = [pltpu.VMEM((e_in if layer is None else d_in, rank), bf16) for layer, _, _ in pieces]
        sent = pl.pallas_call(
            functools.partial(send_kernel, pieces),
            out_shape=jax.ShapeDtypeStruct((n_rows, rank), f32),
            in_specs=[HBM] * 4 + [ANY] * len(after),
            out_specs=VMEM,
            scratch_shapes=acts + projs + [dma((2 * len(pieces),))],
            compiler_params=vmem(8),
        )(expert_act, expert_proj_in, dense_act, dense_proj_in, *after)
        got.append(lax.ppermute(sent, "tensor", swap))
        after = [sent]

    y_d, y_e, own, hot = pl.pallas_call(
        own_kernel,
        out_shape=[
            jax.ShapeDtypeStruct((layers, micro, rows, rank), f32),
            jax.ShapeDtypeStruct((micro, experts, slots, rank), f32),
            jax.ShapeDtypeStruct((micro, rank), f32),
            jax.ShapeDtypeStruct((micro, domains), f32),
        ],
        in_specs=[SMEM] + [HBM] * 10,
        out_specs=[VMEM] * 4,
        scratch_shapes=[
            pltpu.VMEM((layers, micro, rows, d_in), bf16),
            pltpu.VMEM((layers, micro, rows, dwidth), bf16),
            pltpu.VMEM((layers, d_in, rank), bf16),
            pltpu.VMEM((layers, dwidth, rank), bf16),
            pltpu.VMEM((micro, experts, slots, e_in), bf16),
            pltpu.VMEM((micro, experts, slots, dwidth), bf16),
            pltpu.VMEM((e_in, rank), bf16),
            pltpu.VMEM((dwidth, rank), bf16),
            pltpu.VMEM((layers, rank, rank), f32),
            pltpu.VMEM((experts, rank, rank), f32),
            dma(((layers + 1) * (3 + 2 * (micro // GROUP)),)),
        ],
        compiler_params=vmem(32),
        name="own_part",
    )(
        domain_ids, dense_act, dense_cot, dense_proj_in, dense_proj_out,
        expert_act, expert_cot, expert_proj_in, expert_proj_out, dense_valid, expert_valid,
    )

    parts = pl.pallas_call(
        functools.partial(combine_kernel, chunks),
        out_shape=jax.ShapeDtypeStruct((world, domains), f32),
        in_specs=[VMEM] * (4 + len(got)),
        out_specs=VMEM,
        compiler_params=vmem(6),
        name="combine",
    )(own, hot, y_d, y_e, *got)
    parts = lax.all_to_all(parts, AXES, 0, 0, tiled=True)

    share = domains // lax.axis_size("dp")
    lanes = -(-domains // 128) * 128
    out = pl.pallas_call(
        final_kernel,
        out_shape=jax.ShapeDtypeStruct((1, share), f32),
        in_specs=[VMEM, VMEM],
        out_specs=VMEM,
        scratch_shapes=[pltpu.VMEM((1, lanes), f32)],
        compiler_params=vmem(1),
        name="final",
    )(parts, prior_mix.reshape(1, domains))
    return out.reshape(share)


def solution(mesh):
    placed = (
        P(None, "dp", "expert", "tensor"),
        P(None, "dp", ("expert", "tensor"), None),
        P(None, "tensor", None),
        P(),
        P("dp", "expert", None, "tensor"),
        P("dp", "expert", "tensor", None),
        P("tensor", None),
        P(),
        P(),
        P("expert", None, None),
        P("dp"),
        P(),
    )

    return jax.shard_map(per_device, mesh=mesh, in_specs=placed, out_specs=P("dp"), check_vma=False)
```

time: 40.7 us -> 41.3 us (1.015)
  starting transfers between devices: 3.11 us -> 5.06 us
  waiting for transfers between devices: 6.04 us -> 4.92 us
    ppermute x2 -> x3, starting transfers between devices: 3.11 us -> 5.06 us  [per_device(): got.append(lax.ppermute(sent, 'tensor', swap))]
    ppermute x2 -> x3, waiting for transfers between devices: 6.04 us -> 4.92 us  [per_device(): got.append(lax.ppermute(sent, 'tensor', swap))]
    pallas_call x1, Pallas kernels: 11.4 us -> 10.6 us  [per_device(): pl.pallas_call(own_kernel, out_shape=[jax.ShapeDtypeStruct((layers, micro...]
    pallas_call x3 -> x4, Pallas kernels: 5.98 us -> 6.63 us  [the longest x3 6.43 us: per_device(): pl.pallas_call(functools.partial(send_kernel, pieces), out_shape=jax.Shap...]
  transfers between devices with their start and end apart: 2 -> 3, of which waited for: 1 -> 1; matrix products, arithmetic and copies ran while one was open for 0% -> 0% of each run, Pallas kernels for 28% -> 26%
where the time goes in v4:
time: 41.3 us; the launch traced here: 41.1 us
  Pallas kernels  17.9 us (43%)
  blocking collectives  13.1 us (32%)
  starting transfers between devices  5.06 us (12%)
  waiting for transfers between devices  4.92 us (12%)
    all_to_all x1, blocking collectives, per_device(): parts = lax.all_to_all(parts, AXES, 0, 0, tiled=True)  13.1 us
    pallas_call x1, Pallas kernels, per_device(): pl.pallas_call(own_kernel, out_shape=[jax.ShapeDtypeStruct((layers, micro...  10.6 us
    pallas_call x3, Pallas kernels, per_device(): pl.pallas_call(functools.partial(send_kernel, pieces), out_shape=jax.Shap...  6.43 us
    ppermute x3, starting transfers between devices, per_device(): got.append(lax.ppermute(sent, 'tensor', swap))  5.06 us
    ppermute x3, waiting for transfers between devices, per_device(): got.append(lax.ppermute(sent, 'tensor', swap))  4.92 us
  transfers between devices with their start and end apart: 3, of which 1 were waited for; matrix products, arithmetic and copies ran while one was open for 0% of the time, Pallas kernels for 26%

profile of v4, /device:TPU:0, one launch (start us, length us, event | category | flops | bytes accessed | tf_op | source)
XLA Modules:
  0.0 41.1 jit_solution(12357783787892822002)
XLA Ops:
  0.0 1.5 %shard_map.118.rest_0_ = f32[256,128]{1,0:T(8,128)S(1)} custom-call(bf16[4,4,64,1280]{3,2,1,0:T(8,128)(2,1)} %e_act.5, bf16[1280,128]{1,0:T(8,128)(2,1)} %e_proj.5, bf16[2,4,256,1792]{3,2,1,0:T(8,128)(2,1)} %d_act.5, bf16[2,1792,128]{2,1,0:T(8,128)(2,1)} %d_proj.5), custom_call_target="tpu_custom_call" | custom-call | tf_op jit(solution)/shard_map/pallas_call | solution.py:205
  1.5 2.1 %shard_map.119.rest_0_ = f32[512,128]{1,0:T(8,128)S(1)} custom-call(bf16[4,4,64,1280]{3,2,1,0:T(8,128)(2,1)} %e_act.5, bf16[1280,128]{1,0:T(8,128)(2,1)} %e_proj.5, bf16[2,4,256,1792]{3,2,1,0:T(8,128)(2,1)} %d_act.5, bf16[2,1792,128]{2,1,0:T(8,128)(2,1)} %d_proj.5, f32[256,128]{1,0:T(8,128)S(1)} %shard_map.118.rest_0_), custom_call_target="tpu_custom_call" | custom-call | tf_op jit(solution)/shard_map/pallas_call | solution.py:205
  3.6 0.0 copy-start
  3.6 2.8 %shard_map.120 = f32[768,128]{1,0:T(8,128)S(1)} custom-call(bf16[4,4,64,1280]{3,2,1,0:T(8,128)(2,1)} %e_act.5, bf16[1280,128]{1,0:T(8,128)(2,1)} %e_proj.5, bf16[2,4,256,1792]{3,2,1,0:T(8,128)(2,1)} %d_act.5, bf16[2,1792,128]{2,1,0:T(8,128)(2,1)} %d_proj.5, f32[512,128]{1,0:T(8,128)S(1)} %shard_map.119.rest_0_), custom_call_target="tpu_custom_call" | custom-call | tf_op jit(solution)/shard_map/pallas_call | solution.py:205
  6.5 0.0 copy-start.1
  6.5 3.0 %collective-permute-start.2 = (f32[768,128]{1,0:T(8,128)S(1)}, f32[768,128]{1,0:T(8,128)S(1)}, u32[]{:S(2)}, u32[]{:S(2)}) collective-permute-start(f32[768,128]{1,0:T(8,128)S(1)} %shard_map.120), channel_id=1, source_target_pairs={{0,1},{1,0},{2,3},{3,2},{4,5},{5,4},{6,7},{7,6},{8,9},{9,8},{10,11... | collective-permute-start | bytes 1179656 | tf_op jit(solution)/shard_map/ppermute | solution.py:213
  9.5 0.1 collective-permute-start.1
  9.6 1.9 %collective-permute-start = (f32[256,128]{1,0:T(8,128)S(1)}, f32[256,128]{1,0:T(8,128)S(1)}, u32[]{:S(2)}, u32[]{:S(2)}) collective-permute-start(f32[256,128]{1,0:T(8,128)S(1)} %shard_map.118.rest_0_), channel_id=1, source_target_pairs={{0,1},{1,0},{2,3},{3,2},{4,5},{5,4},{6,7},{7,6},{8,9},{9,8},{10,11... | collective-permute-start | bytes 393224 | tf_op jit(solution)/shard_map/ppermute | solution.py:213
  11.5 0.0 copy-done
  11.5 10.6 %own_part.1 = (f32[2,4,128,128]{3,2,1,0:T(8,128)S(1)}, f32[4,4,32,128]{3,2,1,0:T(8,128)S(1)}, f32[4,128]{1,0:T(4,128)S(1)}, f32[4,64]{1,0:T(4,128)S(1)}) custom-call(s32[4]{0:T(128)S(1)} %copy-done, bf16[2,4,256,1792]{3,2,1,0:T(8,128)(2,1)} %d_act.5, bf16[2,4,128,3584]{3,2,1,0:T(8,128)(2,1)} %dcot.1, bf16[2,1792,128]{2,1,0:T(8,128)(2,1)} %d_proj.5, ...), custom_call_target="tpu_custom_call" | custom-call | tf_op jit(solution)/shard_map/own_part/pallas_call | solution.py:216
  22.1 4.9 %collective-permute-done.rest_0_ = f32[256,128]{1,0:T(8,128)S(1)} collective-permute-done((f32[256,128]{1,0:T(8,128)S(1)}, f32[256,128]{1,0:T(8,128)S(1)}, u32[]{:S(2)}, u32[]{:S(2)}) %collective-permute-start) | collective-permute-done | bytes 131104 | tf_op jit(solution)/shard_map/ppermute | solution.py:213
  27.1 0.0 collective-permute-done.1.rest_1_
  27.1 0.0 collective-permute-done.2.rest_2_
  27.1 0.2 combine.1
  27.3 13.1 %all_to_all.11 = f32[32,1,64]{2,1,0:T(1,128)S(1)} all-to-all(f32[32,1,64]{2,1,0:T(1,128)S(1)} %bitcast.6), channel_id=1, replica_groups=mesh['dp'=8,'expert'=2,'tensor'=2] {'dp','expert','tensor'}, dimensions={0} | all-to-all | bytes 16384 | tf_op jit(solution)/shard_map/all_to_all | solution.py:254
  40.4 0.0 copy-done.1
  40.4 0.7 %final.1 = f32[1,8]{1,0:T(1,128)} custom-call(f32[32,64]{1,0:T(8,128)S(1)} %bitcast.7, f32[1,64]{1,0:T(1,128)S(1)} %bitcast.8), custom_call_target="tpu_custom_call" | custom-call | tf_op jit(solution)/shard_map/final/pallas_call | solution.py:258
Async XLA Ops:
  3.6 7.9 %copy-start = (s32[4]{0:T(128)S(1)}, s32[4]{0:T(128)}, u32[]{:S(2)}) copy-start(s32[4]{0:T(128)} %ids.1) | copy-start | bytes 52
  6.5 33.9 %copy-start.1 = (f32[64]{0:T(128)S(1)}, f32[64]{0:T(128)}, u32[]{:S(2)}) copy-start(f32[64]{0:T(128)} %param.23) | copy-start | bytes 772
  6.5 20.6 %collective-permute-start.2 = (f32[768,128]{1,0:T(8,128)S(1)}, f32[768,128]{1,0:T(8,128)S(1)}, u32[]{:S(2)}, u32[]{:S(2)}) collective-permute-start(f32[768,128]{1,0:T(8,128)S(1)} %shard_map.120), channel_id=1, source_target_pairs={{0,1},{1,0},{2,3},{3,2},{4,5},{5,4},{6,7},{7,6},{8,9},{9,8},{10,11... | collective-permute-start | bytes 1179656 | tf_op jit(solution)/shard_map/ppermute | solution.py:213
  9.5 17.6 %collective-permute-start.1 = (f32[512,128]{1,0:T(8,128)S(1)}, f32[512,128]{1,0:T(8,128)S(1)}, u32[]{:S(2)}, u32[]{:S(2)}) collective-permute-start(f32[512,128]{1,0:T(8,128)S(1)} %shard_map.119.rest_0_), channel_id=1, source_target_pairs={{0,1},{1,0},{2,3},{3,2},{4,5},{5,4},{6,7},{7,6},{8,9},{9,8},{10,11... | collective-permute-start | bytes 786440 | tf_op jit(solution)/shard_map/ppermute | solution.py:213
  9.6 17.5 %collective-permute-start = (f32[256,128]{1,0:T(8,128)S(1)}, f32[256,128]{1,0:T(8,128)S(1)}, u32[]{:S(2)}, u32[]{:S(2)}) collective-permute-start(f32[256,128]{1,0:T(8,128)S(1)} %shard_map.118.rest_0_), channel_id=1, source_target_pairs={{0,1},{1,0},{2,3},{3,2},{4,5},{5,4},{6,7},{7,6},{8,9},{9,8},{10,11... | collective-permute-start | bytes 393224 | tf_op jit(solution)/shard_map/ppermute | solution.py:213

commit v5 on v4

--- a/solution.py
+++ b/solution.py
@@ -61,51 +61,71 @@
         start += u.shape[0]
 
 
+def is_second():
+    return lax.axis_index("expert") == lax.axis_size("expert") - 1
+
+
+def expert_kernel(second, eact, ecot, epin, epout, evaldn, *rest):
+    ye, own, eact_v, epin_v, eval_v, sems = rest[-6:]
+    micro, experts, slots, ewidth = eact_v.shape
+    rank = eval_v.shape[-1]
+
+    def work():
+        here = pl.ds(lax.axis_index("tensor") * slots, slots)
+        groups = [pl.ds(g, GROUP) for g in range(0, micro, GROUP)]
+        pairs = [(epin, epin_v), (evaldn, eval_v)]
+        pairs += [(eact.at[g, :, here, :], eact_v.at[g]) for g in groups]
+        copies = iter(start_all(pairs, sems))
+        ws = [
+            dot(ecot[first : first + GROUP].reshape(GROUP * experts * slots, -1), epout[...])
+            for first in range(0, micro, GROUP)
+        ]
+        next(copies).wait()
+        next(copies).wait()
+        for first, w in zip(range(0, micro, GROUP), ws):
+            next(copies).wait()
+            u = dot(eact_v[first : first + GROUP].reshape(GROUP * experts * slots, ewidth), epin_v[...])
+            totals = [jnp.zeros((1, rank), jnp.float32) for _ in range(GROUP)]
+            for e in range(experts):
+                places = [slice((m * experts + e) * slots, (m * experts + e + 1) * slots) for m in range(GROUP)]
+                y = dot_exact(jnp.concatenate([w[place] for place in places], axis=0), eval_v[e])
+                for m in range(GROUP):
+                    y_m = y[m * slots : (m + 1) * slots]
+                    ye[first + m, e] = y_m
+                    totals[m] = totals[m] + jnp.sum(u[places[m]] * y_m, axis=0, keepdims=True)
+            for m in range(GROUP):
+                own[pl.ds(first + m, 1), :] = totals[m]
+
+    def idle():
+        ye[...] = jnp.zeros_like(ye)
+        own[...] = jnp.zeros_like(own)
+
+    lax.cond(is_second() if second else jnp.logical_not(is_second()), work, idle)
+
+
 def own_kernel(
-    ids, dact, dcot, dpin, dpout, eact, ecot, epin, epout, dval, evaldn,
-    yd, ye, own, hot,
-    dact_v, dcot_v, dpin_v, dpout_v, eact_v, ecot_v, epin_v, epout_v, dval_v, eval_v, sems,
+    ids, dact, dcot, dpin, dpout, dval,
+    yd, own, hot,
+    dact_v, dpin_v, dval_v, sems,
 ):
     layers, micro, rows, dwidth = dact_v.shape
-    _, experts, slots, ewidth = eact_v.shape
     rank = dval_v.shape[-1]
-    tensor = lax.axis_index("tensor")
+    here = pl.ds(lax.axis_index("tensor") * rows, rows)
     groups = [pl.ds(g, GROUP) for g in range(0, micro, GROUP)]
-    pairs = [(epout, epout_v), (evaldn, eval_v), (epin, epin_v)]
-    for g in groups:
-        pairs += [
-            (ecot.at[g], ecot_v.at[g]),
-            (eact.at[g, :, pl.ds(tensor * slots, slots), :], eact_v.at[g]),
-        ]
+    pairs = []
     for l in range(layers):
-        pairs += [(dpout.at[l], dpout_v.at[l]), (dval.at[l], dval_v.at[l]), (dpin.at[l], dpin_v.at[l])]
-        for g in groups:
-            pairs += [
-                (dcot.at[l, g], dcot_v.at[l, g]),
-                (dact.at[l, g, pl.ds(tensor * rows, rows), :], dact_v.at[l, g]),
-            ]
+        pairs += [(dval.at[l], dval_v.at[l]), (dpin.at[l], dpin_v.at[l])]
+        pairs += [(dact.at[l, g, here, :], dact_v.at[l, g]) for g in groups]
     copies = iter(start_all(pairs, sems))
     totals = [jnp.zeros((1, rank), jnp.float32) for _ in range(micro)]
-    for _ in range(3):
-        next(copies).wait()
-    for first in range(0, micro, GROUP):
-        next(copies).wait()
-        w = dot(ecot_v[first : first + GROUP].reshape(GROUP * experts * slots, -1), epout_v[...])
-        next(copies).wait()
-        u = dot(eact_v[first : first + GROUP].reshape(GROUP * experts * slots, ewidth), epin_v[...])
-        for e in range(experts):
-            places = [slice((m * experts + e) * slots, (m * experts + e + 1) * slots) for m in range(GROUP)]
-            y = dot_exact(jnp.concatenate([w[place] for place in places], axis=0), eval_v[e])
-            for m in range(GROUP):
-                y_m = y[m * slots : (m + 1) * slots]
-                ye[first + m, e] = y_m
-                totals[first + m] = totals[first + m] + jnp.sum(u[places[m]] * y_m, axis=0, keepdims=True)
     for l in range(layers):
-        for _ in range(3):
-            next(copies).wait()
-        for first in range(0, micro, GROUP):
-            next(copies).wait()
-            w = dot(dcot_v[l, first : first + GROUP].reshape(GROUP * rows, -1), dpout_v[l])
+        w_l = [
+            dot(dcot[l, first : first + GROUP].reshape(GROUP * rows, -1), dpout[l])
+            for first in range(0, micro, GROUP)
+        ]
+        next(copies).wait()
+        next(copies).wait()
+        for first, w in zip(range(0, micro, GROUP), w_l):
             next(copies).wait()
             u = dot(dact_v[l, first : first + GROUP].reshape(GROUP * rows, dwidth), dpin_v[l])
             y = dot_exact(w, dval_v[l])
@@ -119,16 +139,16 @@
         hot[pl.ds(m, 1), :] = (lane == ids[m]).astype(jnp.float32)
 
 
-def combine_kernel(chunks, own, hot, yd, ye, *rest):
+def combine_kernel(chunks, own, hot, yd, ye, own_e, ye_early, own_early, *rest):
     *got, out = rest
     micro, _ = yd.shape[1:3]
     experts, slots, rank = ye.shape[1:]
-    parts = [own[pl.ds(m, 1), :] for m in range(micro)]
+    parts = [own[pl.ds(m, 1), :] + own_e[pl.ds(m, 1), :] + own_early[pl.ds(m, 1), :] for m in range(micro)]
     for pieces, u in zip(chunks, got):
         start = 0
         for layer, first, many in pieces:
             for m in range(first, first + many):
-                y = ye[m].reshape(experts * slots, rank) if layer is None else yd[layer, m]
+                y = (ye[m] + ye_early[m]).reshape(experts * slots, rank) if layer is None else yd[layer, m]
                 part = u[start : start + y.shape[0], :] * y
                 parts[m] = parts[m] + jnp.sum(part, axis=0, keepdims=True)
                 start += y.shape[0]
@@ -166,7 +186,7 @@
     domain_ids,
     prior_mix,
 ):
-    layers, micro, rows, dwidth = dense_cot.shape
+    layers, micro, rows, _ = dense_cot.shape
     experts, slots = expert_cot.shape[1:3]
     d_in = dense_act.shape[3]
     e_in = expert_act.shape[3]
@@ -179,11 +199,12 @@
     dma = pltpu.SemaphoreType.DMA
 
     hbm = functools.partial(pltpu.with_memory_space_constraint, memory_space=pltpu.HBM)
-    dense_act, dense_cot, dense_proj_in, dense_proj_out = map(
-        hbm, (dense_act, dense_cot, dense_proj_in, dense_proj_out)
+    near = functools.partial(pltpu.with_memory_space_constraint, memory_space=pltpu.VMEM)
+    dense_act, dense_proj_in, expert_act, expert_proj_in = map(
+        hbm, (dense_act, dense_proj_in, expert_act, expert_proj_in)
     )
-    expert_act, expert_cot, expert_proj_in, expert_proj_out = map(
-        hbm, (expert_act, expert_cot, expert_proj_in, expert_proj_out)
+    dense_cot, dense_proj_out, expert_cot, expert_proj_out = map(
+        near, (dense_cot, dense_proj_out, expert_cot, expert_proj_out)
     )
     dense_valid, expert_valid = hbm(dense_valid), hbm(expert_valid)
 
@@ -193,15 +214,38 @@
         [(None, half, micro - half), (0, 0, half)],
         [(0, half, micro - half)] + [(l, 0, micro) for l in range(1, layers)],
     ]
+    e_out = [
+        jax.ShapeDtypeStruct((micro, experts, slots, rank), f32),
+        jax.ShapeDtypeStruct((micro, rank), f32),
+    ]
+
+    def expert_part(second, after):
+        return pl.pallas_call(
+            functools.partial(expert_kernel, second),
+            out_shape=e_out,
+            in_specs=[HBM, VMEM, HBM, VMEM, HBM] + [ANY] * len(after),
+            out_specs=[VMEM] * 2,
+            scratch_shapes=[
+                pltpu.VMEM((micro, experts, slots, e_in), bf16),
+                pltpu.VMEM((e_in, rank), bf16),
+                pltpu.VMEM((experts, rank, rank), f32),
+                dma((2 + micro // GROUP,)),
+            ],
+            compiler_params=vmem(12),
+        )(expert_act, expert_cot, expert_proj_in, expert_proj_out, expert_valid, *after)
+
     got = []
     after = []
-    for pieces in chunks:
+    for i, pieces in enumerate(chunks):
         n_rows = sum(many * (experts * slots if layer is None else rows) for layer, _, many in pieces)
         acts = [
             pltpu.VMEM((many, experts, slots, e_in) if layer is None else (many, rows, d_in), bf16)
             for layer, _, many in pieces
         ]
         projs = [pltpu.VMEM((e_in if layer is None else d_in, rank), bf16) for layer, _, _ in pieces]
+        if i == len(chunks) - 1:
+            y_early, own_early = expert_part(True, after)
+            after = [own_early]
         sent = pl.pallas_call(
             functools.partial(send_kernel, pieces),
             out_shape=jax.ShapeDtypeStruct((n_rows, rank), f32),
@@ -213,44 +257,34 @@
         got.append(lax.ppermute(sent, "tensor", swap))
         after = [sent]
 
-    y_d, y_e, own, hot = pl.pallas_call(
+    y_e, own_e = expert_part(False, [sent])
+    y_d, own, hot = pl.pallas_call(
         own_kernel,
         out_shape=[
             jax.ShapeDtypeStruct((layers, micro, rows, rank), f32),
-            jax.ShapeDtypeStruct((micro, experts, slots, rank), f32),
             jax.ShapeDtypeStruct((micro, rank), f32),
             jax.ShapeDtypeStruct((micro, domains), f32),
         ],
-        in_specs=[SMEM] + [HBM] * 10,
-        out_specs=[VMEM] * 4,
+        in_specs=[SMEM, HBM, VMEM, HBM, VMEM, HBM],
+        out_specs=[VMEM] * 3,
         scratch_shapes=[
             pltpu.VMEM((layers, micro, rows, d_in), bf16),
-            pltpu.VMEM((layers, micro, rows, dwidth), bf16),
             pltpu.VMEM((layers, d_in, rank), bf16),
-            pltpu.VMEM((layers, dwidth, rank), bf16),
-            pltpu.VMEM((micro, experts, slots, e_in), bf16),
-            pltpu.VMEM((micro, experts, slots, dwidth), bf16),
-            pltpu.VMEM((e_in, rank), bf16),
-            pltpu.VMEM((dwidth, rank), bf16),
             pltpu.VMEM((layers, rank, rank), f32),
-            pltpu.VMEM((experts, rank, rank), f32),
-            dma(((layers + 1) * (3 + 2 * (micro // GROUP)),)),
+            dma((layers * (2 + micro // GROUP),)),
         ],
-        compiler_params=vmem(32),
+        compiler_params=vmem(20),
         name="own_part",
-    )(
-        domain_ids, dense_act, dense_cot, dense_proj_in, dense_proj_out,
-        expert_act, expert_cot, expert_proj_in, expert_proj_out, dense_valid, expert_valid,
-    )
+    )(domain_ids, dense_act, dense_cot, dense_proj_in, dense_proj_out, dense_valid)
 
     parts = pl.pallas_call(
         functools.partial(combine_kernel, chunks),
         out_shape=jax.ShapeDtypeStruct((world, domains), f32),
-        in_specs=[VMEM] * (4 + len(got)),
+        in_specs=[VMEM] * (7 + len(got)),
         out_specs=VMEM,
         compiler_params=vmem(6),
         name="combine",
-    )(own, hot, y_d, y_e, *got)
+    )(own, hot, y_d, y_e, own_e, y_early, own_early, *got)
     parts = lax.all_to_all(parts, AXES, 0, 0, tiled=True)
 
     share = domains // lax.axis_size("dp")

time: 41.3 us -> 42.9 us (1.039)
  blocking collectives: 13.1 us -> 15.9 us
  Pallas kernels: 17.9 us -> 16.7 us
  local copies, waits for them, and re-layouts: 0.01 us -> 0.78 us
  waiting for transfers between devices: 4.92 us -> 4.16 us
    pallas_call x1, Pallas kernels: 10.6 us -> 5.15 us  [per_device(): pl.pallas_call(own_kernel, out_shape=[jax.ShapeDtypeStruct((layers, micro...]
    pallas_call x0 -> x2, Pallas kernels: none -> 4 us  [expert_part(): pl.pallas_call(functools.partial(expert_kernel, second), out_shape=e_out,...]
    all_to_all x1, blocking collectives: 13.1 us -> 15.9 us  [per_device(): parts = lax.all_to_all(parts, AXES, 0, 0, tiled=True)]
    unnamed x4 -> x14, local copies, waits for them, and re-layouts: 0.01 us -> 0.78 us
    ppermute x3, waiting for transfers between devices: 4.92 us -> 4.16 us  [per_device(): got.append(lax.ppermute(sent, 'tensor', swap))]
  transfers between devices with their start and end apart: 3 -> 3, of which waited for: 1 -> 1; matrix products, arithmetic and copies ran while one was open for 0% -> 0% of each run, Pallas kernels for 26% -> 21%
where the time goes in v5:
time: 42.9 us; the launch traced here: 42.8 us
  Pallas kernels  16.7 us (39%)
  blocking collectives  15.9 us (37%)
  starting transfers between devices  5.06 us (12%)
  waiting for transfers between devices  4.16 us (10%)
  local copies, waits for them, and re-layouts  0.78 us (2%)
    all_to_all x1, blocking collectives, per_device(): parts = lax.all_to_all(parts, AXES, 0, 0, tiled=True)  15.9 us
    pallas_call x3, Pallas kernels, per_device(): pl.pallas_call(functools.partial(send_kernel, pieces), out_shape=jax.Shap...  6.7 us
    pallas_call x1, Pallas kernels, per_device(): pl.pallas_call(own_kernel, out_shape=[jax.ShapeDtypeStruct((layers, micro...  5.15 us
    ppermute x3, starting transfers between devices, per_device(): got.append(lax.ppermute(sent, 'tensor', swap))  5.06 us
    ppermute x3, waiting for transfers between devices, per_device(): got.append(lax.ppermute(sent, 'tensor', swap))  4.16 us
    pallas_call x2, Pallas kernels, expert_part(): pl.pallas_call(functools.partial(expert_kernel, second), out_shape=e_out,...  4 us
  transfers between devices with their start and end apart: 3, of which 1 were waited for; matrix products, arithmetic and copies ran while one was open for 0% of the time, Pallas kernels for 21%

profile of v5, /device:TPU:0, one launch (start us, length us, event | category | flops | bytes accessed | tf_op | source)
XLA Modules:
  0.0 42.8 jit_solution(3581513475587193997)
XLA Ops:
  0.0 1.5 %shard_map.118.rest_0_ = f32[256,128]{1,0:T(8,128)S(1)} custom-call(bf16[4,4,64,1280]{3,2,1,0:T(8,128)(2,1)} %eact.3, bf16[1280,128]{1,0:T(8,128)(2,1)} %epin.3, bf16[2,4,256,1792]{3,2,1,0:T(8,128)(2,1)} %d_act.5, bf16[2,1792,128]{2,1,0:T(8,128)(2,1)} %d_proj.5), custom_call_target="tpu_custom_call" | custom-call | tf_op jit(solution)/shard_map/pallas_call | solution.py:249
  1.5 0.0 copy-start
  1.5 0.0 copy-start.1
  1.6 2.2 %shard_map.119.rest_0_ = f32[512,128]{1,0:T(8,128)S(1)} custom-call(bf16[4,4,64,1280]{3,2,1,0:T(8,128)(2,1)} %eact.3, bf16[1280,128]{1,0:T(8,128)(2,1)} %epin.3, bf16[2,4,256,1792]{3,2,1,0:T(8,128)(2,1)} %d_act.5, bf16[2,1792,128]{2,1,0:T(8,128)(2,1)} %d_proj.5, f32[256,128]{1,0:T(8,128)S(1)} %shard_map.118.rest_0_), custom_call_target="tpu_custom_call" | custom-call | tf_op jit(solution)/shard_map/pallas_call | solution.py:249
  3.8 0.5 %copy-done = bf16[4,4,32,3584]{3,2,1,0:T(8,128)(2,1)S(1)} copy-done((bf16[4,4,32,3584]{3,2,1,0:T(8,128)(2,1)S(1)}, bf16[4,4,32,3584]{3,2,1,0:T(8,128)(2,1)}, u32[]{:S(2)}) %copy-start) | copy-done | bytes 3670040
  4.3 0.2 copy-done.1
  4.5 0.1 shard_map.120
  4.6 0.0 slice-start
  4.6 0.0 slice-start.1
  4.6 3.0 %shard_map.121.rest_0_ = f32[768,128]{1,0:T(8,128)S(1)} custom-call(bf16[4,4,64,1280]{3,2,1,0:T(8,128)(2,1)} %eact.3, bf16[1280,128]{1,0:T(8,128)(2,1)} %epin.3, bf16[2,4,256,1792]{3,2,1,0:T(8,128)(2,1)} %d_act.5, bf16[2,1792,128]{2,1,0:T(8,128)(2,1)} %d_proj.5, f32[4,128]{1,0:T(4,128)S(1)} %get-tuple-element.15.rest_0_.own_early), custom_call_target="tpu_custom_call" | custom-call | tf_op jit(solution)/shard_map/pallas_call | solution.py:249
  7.6 0.0 copy-start.2
  7.6 0.0 copy-start.3
  7.6 3.0 %collective-permute-start.2 = (f32[768,128]{1,0:T(8,128)S(1)}, f32[768,128]{1,0:T(8,128)S(1)}, u32[]{:S(2)}, u32[]{:S(2)}) collective-permute-start(f32[768,128]{1,0:T(8,128)S(1)} %shard_map.121.rest_0_), channel_id=1, source_target_pairs={{0,1},{1,0},{2,3},{3,2},{4,5},{5,4},{6,7},{7,6},{8,9},{9,8},{10,11... | collective-permute-start | bytes 1179656 | tf_op jit(solution)/shard_map/ppermute | solution.py:257
  10.6 0.1 collective-permute-start.1
  10.7 1.9 %collective-permute-start = (f32[256,128]{1,0:T(8,128)S(1)}, f32[256,128]{1,0:T(8,128)S(1)}, u32[]{:S(2)}, u32[]{:S(2)}) collective-permute-start(f32[256,128]{1,0:T(8,128)S(1)} %shard_map.118.rest_0_), channel_id=1, source_target_pairs={{0,1},{1,0},{2,3},{3,2},{4,5},{5,4},{6,7},{7,6},{8,9},{9,8},{10,11... | collective-permute-start | bytes 393224 | tf_op jit(solution)/shard_map/ppermute | solution.py:257
  12.7 3.9 %shard_map.122 = (f32[4,4,32,128]{3,2,1,0:T(8,128)S(1)}, f32[4,128]{1,0:T(4,128)S(1)}) custom-call(bf16[4,4,64,1280]{3,2,1,0:T(8,128)(2,1)} %eact.3, bf16[4,4,32,3584]{3,2,1,0:T(8,128)(2,1)S(1)} %copy-done, bf16[1280,128]{1,0:T(8,128)(2,1)} %epin.3, bf16[3584,128]{1,0:T(8,128)(2,1)S(1)} %copy-done.1, f32[4,128,128]{2,1,0:T(8,128)} %evaldn.3, ...), custom_call_target="tpu_custom_call" | custom-call | tf_op jit(solution)/shard_map/pallas_call | solution.py:223
  16.6 0.0 slice-done
  16.6 0.0 slice-done.1
  16.6 0.0 copy-done.2
  16.6 0.0 copy-done.3
  16.7 0.0 copy-start.4
  16.7 5.2 %own_part.1 = (f32[2,4,128,128]{3,2,1,0:T(8,128)S(1)}, f32[4,128]{1,0:T(4,128)S(1)}, f32[4,64]{1,0:T(4,128)S(1)}) custom-call(s32[4]{0:T(128)S(1)} %copy-done.3, bf16[2,4,256,1792]{3,2,1,0:T(8,128)(2,1)} %d_act.5, bf16[2,4,128,3584]{3,2,1,0:T(8,128)(2,1)S(1)} %bitcast.7, bf16[2,1792,128]{2,1,0:T(8,128)(2,1)} %d_proj.5, bf16[2,3584,128]{2,1,0:T(8,128)(2,1)S(1)} %copy-done.2, ...), custom_call_target="tpu_custom_call" | custom-call | tf_op jit(solution)/shard_map/own_part/pallas_call | solution.py:261
  21.8 4.2 %collective-permute-done.rest_0_ = f32[256,128]{1,0:T(8,128)S(1)} collective-permute-done((f32[256,128]{1,0:T(8,128)S(1)}, f32[256,128]{1,0:T(8,128)S(1)}, u32[]{:S(2)}, u32[]{:S(2)}) %collective-permute-start) | collective-permute-done | bytes 131104 | tf_op jit(solution)/shard_map/ppermute | solution.py:257
  26.0 0.0 collective-permute-done.1.rest_1_
  26.0 0.0 collective-permute-done.2.rest_2_
  26.0 0.2 combine.1
  26.2 15.9 %all_to_all.11 = f32[32,1,64]{2,1,0:T(1,128)S(1)} all-to-all(f32[32,1,64]{2,1,0:T(1,128)S(1)} %bitcast.8), channel_id=1, replica_groups=mesh['dp'=8,'expert'=2,'tensor'=2] {'dp','expert','tensor'}, dimensions={0} | all-to-all | bytes 16384 | tf_op jit(solution)/shard_map/all_to_all | solution.py:288
  42.0 0.0 copy-done.4
  42.1 0.7 %final.1 = f32[1,8]{1,0:T(1,128)} custom-call(f32[32,64]{1,0:T(8,128)S(1)} %bitcast.9, f32[1,64]{1,0:T(1,128)S(1)} %bitcast.10), custom_call_target="tpu_custom_call" | custom-call | tf_op jit(solution)/shard_map/final/pallas_call | solution.py:292
  (1 shorter events, 0.0 us)
Async XLA Ops:
  1.5 2.8 %copy-start = (bf16[4,4,32,3584]{3,2,1,0:T(8,128)(2,1)S(1)}, bf16[4,4,32,3584]{3,2,1,0:T(8,128)(2,1)}, u32[]{:S(2)}) copy-start(bf16[4,4,32,3584]{3,2,1,0:T(8,128)(2,1)} %ecot.3) | copy-start | bytes 11010052
  1.5 3.0 %copy-start.1 = (bf16[3584,128]{1,0:T(8,128)(2,1)S(1)}, bf16[3584,128]{1,0:T(8,128)(2,1)}, u32[]{:S(2)}) copy-start(bf16[3584,128]{1,0:T(8,128)(2,1)} %epout.3) | copy-start | bytes 2752516
  4.6 12.0 %slice-start = ((s8[7340032]{0:T(1024)(128)(4,1)}), s8[4194304]{0:T(1024)(128)(4,1)S(1)}, s32[]{:S(2)}) async-start(s8[7340032]{0:T(1024)(128)(4,1)} %bitcast.6), calls=%async_computation.1 | async-start | bytes 8388608
  4.6 12.0 %slice-start.1 = ((s8[7340032]{0:T(1024)(128)(4,1)}), s8[3145728]{0:T(1024)(128)(4,1)S(1)}, s32[]{:S(2)}) async-start(s8[7340032]{0:T(1024)(128)(4,1)} %bitcast.6), calls=%async_computation.2 | async-start | bytes 6291456
  7.6 9.1 %copy-start.2 = (bf16[2,3584,128]{2,1,0:T(8,128)(2,1)S(1)}, bf16[2,3584,128]{2,1,0:T(8,128)(2,1)}, u32[]{:S(2)}) copy-start(bf16[2,3584,128]{2,1,0:T(8,128)(2,1)} %dpout.1) | copy-start | bytes 5505028
  7.6 9.1 %copy-start.3 = (s32[4]{0:T(128)S(1)}, s32[4]{0:T(128)}, u32[]{:S(2)}) copy-start(s32[4]{0:T(128)} %ids.1) | copy-start | bytes 52
  7.6 18.4 %collective-permute-start.2 = (f32[768,128]{1,0:T(8,128)S(1)}, f32[768,128]{1,0:T(8,128)S(1)}, u32[]{:S(2)}, u32[]{:S(2)}) collective-permute-start(f32[768,128]{1,0:T(8,128)S(1)} %shard_map.121.rest_0_), channel_id=1, source_target_pairs={{0,1},{1,0},{2,3},{3,2},{4,5},{5,4},{6,7},{7,6},{8,9},{9,8},{10,11... | collective-permute-start | bytes 1179656 | tf_op jit(solution)/shard_map/ppermute | solution.py:257
  10.6 15.4 %collective-permute-start.1 = (f32[512,128]{1,0:T(8,128)S(1)}, f32[512,128]{1,0:T(8,128)S(1)}, u32[]{:S(2)}, u32[]{:S(2)}) collective-permute-start(f32[512,128]{1,0:T(8,128)S(1)} %shard_map.119.rest_0_), channel_id=1, source_target_pairs={{0,1},{1,0},{2,3},{3,2},{4,5},{5,4},{6,7},{7,6},{8,9},{9,8},{10,11... | collective-permute-start | bytes 786440 | tf_op jit(solution)/shard_map/ppermute | solution.py:257
  10.7 15.3 %collective-permute-start = (f32[256,128]{1,0:T(8,128)S(1)}, f32[256,128]{1,0:T(8,128)S(1)}, u32[]{:S(2)}, u32[]{:S(2)}) collective-permute-start(f32[256,128]{1,0:T(8,128)S(1)} %shard_map.118.rest_0_), channel_id=1, source_target_pairs={{0,1},{1,0},{2,3},{3,2},{4,5},{5,4},{6,7},{7,6},{8,9},{9,8},{10,11... | collective-permute-start | bytes 393224 | tf_op jit(solution)/shard_map/ppermute | solution.py:257
  16.7 25.4 %copy-start.4 = (f32[64]{0:T(128)S(1)}, f32[64]{0:T(128)}, u32[]{:S(2)}) copy-start(f32[64]{0:T(128)} %param.23) | copy-start | bytes 772

commit v6 on v5

--- a/solution.py
+++ b/solution.py
@@ -139,19 +139,29 @@
         hot[pl.ds(m, 1), :] = (lane == ids[m]).astype(jnp.float32)
 
 
-def combine_kernel(chunks, own, hot, yd, ye, own_e, ye_early, own_early, *rest):
-    *got, out = rest
-    micro, _ = yd.shape[1:3]
-    experts, slots, rank = ye.shape[1:]
-    parts = [own[pl.ds(m, 1), :] + own_e[pl.ds(m, 1), :] + own_early[pl.ds(m, 1), :] for m in range(micro)]
+def received(chunks, got, parts, yd, y_expert):
     for pieces, u in zip(chunks, got):
         start = 0
         for layer, first, many in pieces:
             for m in range(first, first + many):
-                y = (ye[m] + ye_early[m]).reshape(experts * slots, rank) if layer is None else yd[layer, m]
+                y = y_expert(m) if layer is None else yd[layer, m]
                 part = u[start : start + y.shape[0], :] * y
                 parts[m] = parts[m] + jnp.sum(part, axis=0, keepdims=True)
                 start += y.shape[0]
+    return parts
+
+
+def gather_kernel(chunks, own, yd, ye, own_e, ye_early, own_early, *rest):
+    *got, out = rest
+    micro, experts, slots, rank = ye.shape
+    parts = [own[pl.ds(m, 1), :] + own_e[pl.ds(m, 1), :] + own_early[pl.ds(m, 1), :] for m in range(micro)]
+    y_expert = lambda m: (ye[m] + ye_early[m]).reshape(experts * slots, rank)
+    out[...] = jnp.concatenate(received(chunks, got, parts, yd, y_expert), axis=0)
+
+
+def combine_kernel(chunk, own, hot, yd, got, out):
+    micro = yd.shape[1]
+    parts = received([chunk], [got], [own[pl.ds(m, 1), :] for m in range(micro)], yd, None)
     scores = jnp.sum(jnp.concatenate(parts, axis=0), axis=1, keepdims=True)
     total = jnp.sum(scores * hot[...], axis=0, keepdims=True)
     out[...] = jnp.broadcast_to(total, out.shape)
@@ -161,11 +171,10 @@
     domains = prior.shape[-1]
     share = out.shape[-1]
     total = jnp.sum(parts[...], axis=0, keepdims=True)
-    spread = jnp.sqrt(jnp.mean(total * total, axis=1, keepdims=True) + 1e-06)
-    half = 0.5 * (total / spread)
+    per_spread = lax.rsqrt(jnp.mean(total * total, axis=1, keepdims=True) + 1e-06)
+    half = total * (0.5 * per_spread)
     mass = jnp.sum(prior[...] * jnp.exp(half), axis=1, keepdims=True)
     lanes = wide.shape[-1]
-    wide[...] = jnp.zeros_like(wide)
     wide[:, :domains] = jnp.log(prior[...]) + half
     first = lax.axis_index("dp") * share
     rolled = pltpu.roll(wide[...], lax.rem(lanes - first, lanes), 1)
@@ -277,14 +286,22 @@
         name="own_part",
     )(domain_ids, dense_act, dense_cot, dense_proj_in, dense_proj_out, dense_valid)
 
+    own = pl.pallas_call(
+        functools.partial(gather_kernel, chunks[:-1]),
+        out_shape=jax.ShapeDtypeStruct((micro, rank), f32),
+        in_specs=[VMEM] * (6 + len(got) - 1),
+        out_specs=VMEM,
+        compiler_params=vmem(6),
+        name="gather",
+    )(own, y_d, y_e, own_e, y_early, own_early, *got[:-1])
     parts = pl.pallas_call(
-        functools.partial(combine_kernel, chunks),
+        functools.partial(combine_kernel, chunks[-1]),
         out_shape=jax.ShapeDtypeStruct((world, domains), f32),
-        in_specs=[VMEM] * (7 + len(got)),
+        in_specs=[VMEM] * 4,
         out_specs=VMEM,
         compiler_params=vmem(6),
         name="combine",
-    )(own, hot, y_d, y_e, own_e, y_early, own_early, *got)
+    )(own, hot, y_d, got[-1])
     parts = lax.all_to_all(parts, AXES, 0, 0, tiled=True)
 
     share = domains // lax.axis_size("dp")

time: 42.9 us -> 43 us (level)
  no operation moved by 1% of the time
where the time goes in v6:
time: 43 us; the launch traced here: 42.8 us
  Pallas kernels  16.8 us (39%)
  blocking collectives  15.9 us (37%)
  starting transfers between devices  5.06 us (12%)
  waiting for transfers between devices  4.16 us (10%)
  local copies, waits for them, and re-layouts  0.78 us (2%)
    all_to_all x1, blocking collectives, per_device(): parts = lax.all_to_all(parts, AXES, 0, 0, tiled=True)  15.9 us
    pallas_call x3, Pallas kernels, per_device(): pl.pallas_call(functools.partial(send_kernel, pieces), out_shape=jax.Shap...  6.7 us
    pallas_call x1, Pallas kernels, per_device(): pl.pallas_call(own_kernel, out_shape=[jax.ShapeDtypeStruct((layers, micro...  5.15 us
    ppermute x3, starting transfers between devices, per_device(): got.append(lax.ppermute(sent, 'tensor', swap))  5.06 us
    ppermute x3, waiting for transfers between devices, per_device(): got.append(lax.ppermute(sent, 'tensor', swap))  4.16 us
    pallas_call x2, Pallas kernels, expert_part(): pl.pallas_call(functools.partial(expert_kernel, second), out_shape=e_out,...  4 us
  transfers between devices with their start and end apart: 3, of which 1 were waited for; matrix products, arithmetic and copies ran while one was open for 0% of the time, Pallas kernels for 21%

profile of v6, /device:TPU:0, one launch (start us, length us, event | category | flops | bytes accessed | tf_op | source)
XLA Modules:
  0.0 42.8 jit_solution(13094683269648273943)
XLA Ops:
  0.0 1.5 %shard_map.118.rest_0_ = f32[256,128]{1,0:T(8,128)S(1)} custom-call(bf16[4,4,64,1280]{3,2,1,0:T(8,128)(2,1)} %eact.3, bf16[1280,128]{1,0:T(8,128)(2,1)} %epin.3, bf16[2,4,256,1792]{3,2,1,0:T(8,128)(2,1)} %d_act.5, bf16[2,1792,128]{2,1,0:T(8,128)(2,1)} %d_proj.5), custom_call_target="tpu_custom_call" | custom-call | tf_op jit(solution)/shard_map/pallas_call | solution.py:258
  1.5 0.0 copy-start
  1.5 0.0 copy-start.1
  1.6 2.2 %shard_map.119.rest_0_ = f32[512,128]{1,0:T(8,128)S(1)} custom-call(bf16[4,4,64,1280]{3,2,1,0:T(8,128)(2,1)} %eact.3, bf16[1280,128]{1,0:T(8,128)(2,1)} %epin.3, bf16[2,4,256,1792]{3,2,1,0:T(8,128)(2,1)} %d_act.5, bf16[2,1792,128]{2,1,0:T(8,128)(2,1)} %d_proj.5, f32[256,128]{1,0:T(8,128)S(1)} %shard_map.118.rest_0_), custom_call_target="tpu_custom_call" | custom-call | tf_op jit(solution)/shard_map/pallas_call | solution.py:258
  3.8 0.5 %copy-done = bf16[4,4,32,3584]{3,2,1,0:T(8,128)(2,1)S(1)} copy-done((bf16[4,4,32,3584]{3,2,1,0:T(8,128)(2,1)S(1)}, bf16[4,4,32,3584]{3,2,1,0:T(8,128)(2,1)}, u32[]{:S(2)}) %copy-start) | copy-done | bytes 3670040
  4.3 0.2 copy-done.1
  4.5 0.1 shard_map.120
  4.6 0.0 slice-start
  4.6 0.0 slice-start.1
  4.6 3.0 %shard_map.121.rest_0_ = f32[768,128]{1,0:T(8,128)S(1)} custom-call(bf16[4,4,64,1280]{3,2,1,0:T(8,128)(2,1)} %eact.3, bf16[1280,128]{1,0:T(8,128)(2,1)} %epin.3, bf16[2,4,256,1792]{3,2,1,0:T(8,128)(2,1)} %d_act.5, bf16[2,1792,128]{2,1,0:T(8,128)(2,1)} %d_proj.5, f32[4,128]{1,0:T(4,128)S(1)} %get-tuple-element.14.rest_0_.own_early), custom_call_target="tpu_custom_call" | custom-call | tf_op jit(solution)/shard_map/pallas_call | solution.py:258
  7.6 0.0 copy-start.2
  7.6 0.0 copy-start.3
  7.6 3.0 %collective-permute-start.2 = (f32[768,128]{1,0:T(8,128)S(1)}, f32[768,128]{1,0:T(8,128)S(1)}, u32[]{:S(2)}, u32[]{:S(2)}) collective-permute-start(f32[768,128]{1,0:T(8,128)S(1)} %shard_map.121.rest_0_), channel_id=1, source_target_pairs={{0,1},{1,0},{2,3},{3,2},{4,5},{5,4},{6,7},{7,6},{8,9},{9,8},{10,11... | collective-permute-start | bytes 1179656 | tf_op jit(solution)/shard_map/ppermute | solution.py:266
  10.6 0.1 collective-permute-start.1
  10.7 1.9 %collective-permute-start = (f32[256,128]{1,0:T(8,128)S(1)}, f32[256,128]{1,0:T(8,128)S(1)}, u32[]{:S(2)}, u32[]{:S(2)}) collective-permute-start(f32[256,128]{1,0:T(8,128)S(1)} %shard_map.118.rest_0_), channel_id=1, source_target_pairs={{0,1},{1,0},{2,3},{3,2},{4,5},{5,4},{6,7},{7,6},{8,9},{9,8},{10,11... | collective-permute-start | bytes 393224 | tf_op jit(solution)/shard_map/ppermute | solution.py:266
  12.7 3.9 %shard_map.122 = (f32[4,4,32,128]{3,2,1,0:T(8,128)S(1)}, f32[4,128]{1,0:T(4,128)S(1)}) custom-call(bf16[4,4,64,1280]{3,2,1,0:T(8,128)(2,1)} %eact.3, bf16[4,4,32,3584]{3,2,1,0:T(8,128)(2,1)S(1)} %copy-done, bf16[1280,128]{1,0:T(8,128)(2,1)} %epin.3, bf16[3584,128]{1,0:T(8,128)(2,1)S(1)} %copy-done.1, f32[4,128,128]{2,1,0:T(8,128)} %evaldn.3, ...), custom_call_target="tpu_custom_call" | custom-call | tf_op jit(solution)/shard_map/pallas_call | solution.py:232
  16.6 0.0 slice-done
  16.6 0.0 slice-done.1
  16.6 0.0 copy-done.2
  16.6 0.0 copy-done.3
  16.7 0.0 copy-start.4
  16.7 5.2 %own_part.1 = (f32[2,4,128,128]{3,2,1,0:T(8,128)S(1)}, f32[4,128]{1,0:T(4,128)S(1)}, f32[4,64]{1,0:T(4,128)S(1)}) custom-call(s32[4]{0:T(128)S(1)} %copy-done.3, bf16[2,4,256,1792]{3,2,1,0:T(8,128)(2,1)} %d_act.5, bf16[2,4,128,3584]{3,2,1,0:T(8,128)(2,1)S(1)} %bitcast.7, bf16[2,1792,128]{2,1,0:T(8,128)(2,1)} %d_proj.5, bf16[2,3584,128]{2,1,0:T(8,128)(2,1)S(1)} %copy-done.2, ...), custom_call_target="tpu_custom_call" | custom-call | tf_op jit(solution)/shard_map/own_part/pallas_call | solution.py:270
  21.8 4.2 %collective-permute-done.rest_0_ = f32[256,128]{1,0:T(8,128)S(1)} collective-permute-done((f32[256,128]{1,0:T(8,128)S(1)}, f32[256,128]{1,0:T(8,128)S(1)}, u32[]{:S(2)}, u32[]{:S(2)}) %collective-permute-start) | collective-permute-done | bytes 131104 | tf_op jit(solution)/shard_map/ppermute | solution.py:266
  26.0 0.0 collective-permute-done.1.rest_1_
  26.0 0.1 gather.1.own
  26.1 0.0 collective-permute-done.2.got
  26.1 0.1 combine.1
  26.2 15.9 %all_to_all.11 = f32[32,1,64]{2,1,0:T(1,128)S(1)} all-to-all(f32[32,1,64]{2,1,0:T(1,128)S(1)} %bitcast.8), channel_id=1, replica_groups=mesh['dp'=8,'expert'=2,'tensor'=2] {'dp','expert','tensor'}, dimensions={0} | all-to-all | bytes 16384 | tf_op jit(solution)/shard_map/all_to_all | solution.py:305
  42.1 0.0 copy-done.4
  42.1 0.7 %final.1 = f32[1,8]{1,0:T(1,128)} custom-call(f32[32,64]{1,0:T(8,128)S(1)} %bitcast.9, f32[1,64]{1,0:T(1,128)S(1)} %bitcast.10), custom_call_target="tpu_custom_call" | custom-call | tf_op jit(solution)/shard_map/final/pallas_call | solution.py:309
  (1 shorter events, 0.0 us)
Async XLA Ops:
  1.5 2.8 %copy-start = (bf16[4,4,32,3584]{3,2,1,0:T(8,128)(2,1)S(1)}, bf16[4,4,32,3584]{3,2,1,0:T(8,128)(2,1)}, u32[]{:S(2)}) copy-start(bf16[4,4,32,3584]{3,2,1,0:T(8,128)(2,1)} %ecot.3) | copy-start | bytes 11010052
  1.5 3.0 %copy-start.1 = (bf16[3584,128]{1,0:T(8,128)(2,1)S(1)}, bf16[3584,128]{1,0:T(8,128)(2,1)}, u32[]{:S(2)}) copy-start(bf16[3584,128]{1,0:T(8,128)(2,1)} %epout.3) | copy-start | bytes 2752516
  4.6 12.0 %slice-start = ((s8[7340032]{0:T(1024)(128)(4,1)}), s8[4194304]{0:T(1024)(128)(4,1)S(1)}, s32[]{:S(2)}) async-start(s8[7340032]{0:T(1024)(128)(4,1)} %bitcast.6), calls=%async_computation.1 | async-start | bytes 8388608
  4.6 12.0 %slice-start.1 = ((s8[7340032]{0:T(1024)(128)(4,1)}), s8[3145728]{0:T(1024)(128)(4,1)S(1)}, s32[]{:S(2)}) async-start(s8[7340032]{0:T(1024)(128)(4,1)} %bitcast.6), calls=%async_computation.2 | async-start | bytes 6291456
  7.6 9.1 %copy-start.2 = (bf16[2,3584,128]{2,1,0:T(8,128)(2,1)S(1)}, bf16[2,3584,128]{2,1,0:T(8,128)(2,1)}, u32[]{:S(2)}) copy-start(bf16[2,3584,128]{2,1,0:T(8,128)(2,1)} %dpout.1) | copy-start | bytes 5505028
  7.6 9.1 %copy-start.3 = (s32[4]{0:T(128)S(1)}, s32[4]{0:T(128)}, u32[]{:S(2)}) copy-start(s32[4]{0:T(128)} %ids.1) | copy-start | bytes 52
  7.6 18.5 %collective-permute-start.2 = (f32[768,128]{1,0:T(8,128)S(1)}, f32[768,128]{1,0:T(8,128)S(1)}, u32[]{:S(2)}, u32[]{:S(2)}) collective-permute-start(f32[768,128]{1,0:T(8,128)S(1)} %shard_map.121.rest_0_), channel_id=1, source_target_pairs={{0,1},{1,0},{2,3},{3,2},{4,5},{5,4},{6,7},{7,6},{8,9},{9,8},{10,11... | collective-permute-start | bytes 1179656 | tf_op jit(solution)/shard_map/ppermute | solution.py:266
  10.6 15.4 %collective-permute-start.1 = (f32[512,128]{1,0:T(8,128)S(1)}, f32[512,128]{1,0:T(8,128)S(1)}, u32[]{:S(2)}, u32[]{:S(2)}) collective-permute-start(f32[512,128]{1,0:T(8,128)S(1)} %shard_map.119.rest_0_), channel_id=1, source_target_pairs={{0,1},{1,0},{2,3},{3,2},{4,5},{5,4},{6,7},{7,6},{8,9},{9,8},{10,11... | collective-permute-start | bytes 786440 | tf_op jit(solution)/shard_map/ppermute | solution.py:266
  10.7 15.3 %collective-permute-start = (f32[256,128]{1,0:T(8,128)S(1)}, f32[256,128]{1,0:T(8,128)S(1)}, u32[]{:S(2)}, u32[]{:S(2)}) collective-permute-start(f32[256,128]{1,0:T(8,128)S(1)} %shard_map.118.rest_0_), channel_id=1, source_target_pairs={{0,1},{1,0},{2,3},{3,2},{4,5},{5,4},{6,7},{7,6},{8,9},{9,8},{10,11... | collective-permute-start | bytes 393224 | tf_op jit(solution)/shard_map/ppermute | solution.py:266
  16.7 25.4 %copy-start.4 = (f32[64]{0:T(128)S(1)}, f32[64]{0:T(128)}, u32[]{:S(2)}) copy-start(f32[64]{0:T(128)} %param.23) | copy-start | bytes 772
